TPU v7x, 32 devices: a whole 2x2x4 slice. The times are simulated.
32 devices in a mesh: blk: 16 (over z, x, core), quarter: 2 (over y).
Axes of the slice: x: 2, y: 2, z: 4, core: 2. Of those that a mesh axis runs over, the one named last changes fastest.
Arguments:
- sensor: bfloat16 [1024, 1024], P(('blk', 'quarter')), may hold values from -24 to 24
- video: bfloat16 [1024, 1024], P(('blk', 'quarter')), may hold values from -24 to 24
- sens_ref: bfloat16 [1024, 1024], replicated, may hold values from -0.25 to 0.25
- vid_ref: bfloat16 [1024, 1024], replicated, may hold values from -0.25 to 0.25
- sens_val: bfloat16 [1024, 1024], replicated, may hold values from -0.1875 to 0.1875
- vid_val: bfloat16 [1024, 1024], replicated, may hold values from -0.1875 to 0.1875
- sens_out: bfloat16 [1024, 1024], replicated, may hold values from -0.1875 to 0.1875
- vid_out: bfloat16 [1024, 1024], replicated, may hold values from -0.1875 to 0.1875
- sens_gain: float32 [1024], replicated, may hold values from 0.5 to 1.5
- vid_gain: float32 [1024], replicated, may hold values from 0.5 to 1.5
Outputs:
- sensor_next: bfloat16 [1024, 1024], P(('blk', 'quarter'))
- video_next: bfloat16 [1024, 1024], P(('blk', 'quarter'))
All inputs are finite; a program needn't handle non-finite values.
Results may differ from a plain program's by a relative error of at most 0.0099.
Values may be sent and summed in bfloat16 or wider, within the bound.
No kernel may reach another device: no remote copies, remote signals or barrier semaphores. Data moves between devices by JAX's collectives and lax.ppermute only.
A program may use at most 64 MiB of HBM per device.

v0:
```python
import jax
import jax.numpy as jnp
from jax import lax
from jax.sharding import PartitionSpec as P

H = 16


def shortened(x):

    def short(part):
        return part.astype(jnp.bfloat16) if part.dtype == jnp.float32 else part

    return jax.tree.map(short, x)


def shifted(x, axis, by):
    peers = lax.axis_size(axis)
    return lax.ppermute(x, axis, [(i, (i + by) % peers) for i in range(peers)])


def project(inputs, weight):
    return jnp.dot(inputs, weight, preferred_element_type=jnp.float32).astype(jnp.bfloat16)


def finish(inputs, mixed, gain, weight):
    power = jnp.mean(mixed * mixed, axis=-1, keepdims=True)
    normed = (mixed * lax.rsqrt(power + 1e-06) * gain).astype(jnp.bfloat16)
    update = jnp.dot(normed, weight, preferred_element_type=jnp.float32)
    return (inputs.astype(jnp.float32) + update).astype(jnp.bfloat16)


def local(
    sensor, video, sens_ref, vid_ref, sens_val, vid_val, sens_out, vid_out, sens_gain, vid_gain
):
    row_count = sensor.shape[0]
    model_width = sensor.shape[1]
    head_count = H
    head_size = model_width // head_count
    score_scale = head_size ** (-0.5)
    sens_r = project(sensor, sens_ref)
    sens_u = project(sensor, sens_val)
    vid_r = project(video, vid_ref)
    vid_u = project(video, vid_val)
    block_ref, block_val = (
        lax.all_gather(sens_r, "quarter", axis=0, tiled=True),
        lax.all_gather(sens_u, "quarter", axis=0, tiled=True),
    )
    block_rows = block_ref.shape[0]
    sens_ref3 = block_ref.reshape(block_rows, head_count, head_size)
    sens_val3 = block_val.reshape(block_rows, head_count, head_size)

    def widen(factors):
        return jnp.repeat(factors, head_size, axis=-1)

    def visit(tile_pair, video_acc, sensor_acc):
        tile_ref, tile_val = tile_pair
        vid_top, vid_total, vid_numer = video_acc
        sens_top, sens_total, sens_numer = sensor_acc
        tile_rows = tile_ref.shape[0]
        scores = (
            jnp.einsum(
                "vhd,shd->hvs",
                tile_ref.reshape(tile_rows, head_count, head_size),
                sens_ref3,
                preferred_element_type=jnp.float32,
            )
            * score_scale
        )
        new_sens_top = jnp.maximum(sens_top, jnp.max(scores, axis=1))
        sens_fade = jnp.exp(sens_top - new_sens_top)
        sens_weights = jnp.exp(scores - new_sens_top[:, None, :])
        sens_total = sens_total * sens_fade + jnp.sum(sens_weights, axis=1)
        sens_term = jnp.einsum(
            "hvs,vhd->shd",
            sens_weights.astype(jnp.bfloat16),
            tile_val.reshape(tile_rows, head_count, head_size),
            preferred_element_type=jnp.float32,
        )
        sens_numer = sens_numer * widen(sens_fade.T) + sens_term.reshape(block_rows, model_width)
        new_vid_top = jnp.maximum(vid_top, jnp.max(scores, axis=2))
        vid_fade = jnp.exp(vid_top - new_vid_top)
        vid_weights = jnp.exp(scores - new_vid_top[:, :, None])
        vid_total = vid_total * vid_fade + jnp.sum(vid_weights, axis=2)
        vid_term = jnp.einsum(
            "hvs,shd->vhd",
            vid_weights.astype(jnp.bfloat16),
            sens_val3,
            preferred_element_type=jnp.float32,
        )
        vid_numer = vid_numer * widen(vid_fade.T) + vid_term.reshape(tile_rows, model_width)
        return ((new_vid_top, vid_total, vid_numer), (new_sens_top, sens_total, sens_numer))

    sensor_start = (
        jnp.full((head_count, block_rows), -1e30, jnp.float32),
        jnp.zeros((head_count, block_rows), jnp.float32),
        jnp.zeros((block_rows, model_width), jnp.float32),
    )
    cycle_turns = lax.axis_size("blk")

    def turn(turn_index, carry):
        tile_pair, video_acc, sensor_acc = carry
        video_acc, sensor_acc = visit(tile_pair, video_acc, sensor_acc)
        tile_pair = jax.tree.map(
            lambda part, own: part.astype(own.dtype),
            shifted(shortened(tile_pair), "blk", 1),
            tile_pair,
        )
        video_acc = shifted((video_acc[0], video_acc[1], video_acc[2]), "blk", 1)
        return (tile_pair, video_acc, sensor_acc)

    carry = lax.fori_loop(
        0,
        cycle_turns,
        turn,
        (
            (vid_r, vid_u),
            (
                jnp.full((head_count, row_count), -1e30, jnp.float32),
                jnp.zeros((head_count, row_count), jnp.float32),
                jnp.zeros((row_count, model_width), jnp.float32),
            ),
            sensor_start,
        ),
    )
    vid_top, vid_total, vid_numer = carry[1]
    sensor_acc = carry[2]
    vid_attn = vid_numer / widen(vid_total.T)
    sens_top, sens_total, sens_numer = sensor_acc
    part_count = lax.axis_size("quarter")
    top_parts = sens_top.reshape(head_count, part_count, row_count).transpose(1, 0, 2)
    total_parts = sens_total.reshape(head_count, part_count, row_count).transpose(1, 0, 2)
    numer_parts = sens_numer.reshape(part_count, row_count, model_width)
    top_parts, total_parts, numer_parts = (
        lax.all_to_all(top_parts, "quarter", split_axis=0, concat_axis=0, tiled=True),
        lax.all_to_all(total_parts, "quarter", split_axis=0, concat_axis=0, tiled=True),
        lax.all_to_all(numer_parts, "quarter", split_axis=0, concat_axis=0, tiled=True),
    )
    joint_top = jnp.max(top_parts, axis=0)
    fades = jnp.exp(top_parts - joint_top[None])
    joint_total = jnp.sum(total_parts * fades, axis=0)
    joint_numer = jnp.sum(numer_parts * widen(fades.transpose(0, 2, 1)), axis=0)
    sens_attn = joint_numer / widen(joint_total.T)
    return (
        finish(sensor, sens_attn, sens_gain, sens_out),
        finish(video, vid_attn, vid_gain, vid_out),
    )


def solution(mesh):
    return jax.shard_map(
        local,
        mesh=mesh,
        in_specs=(
            P(("blk", "quarter"), None),
            P(("blk", "quarter"), None),
            P(),
            P(),
            P(),
            P(),
            P(),
            P(),
            P(),
            P(),
        ),
        out_specs=(P(("blk", "quarter"), None), P(("blk", "quarter"), None)),
        check_vma=False,
    )
```

profile of v0, /device:TPU:0, one launch (start us, length us, event | category | flops | bytes accessed | tf_op | source)
XLA Modules:
  0.0 317.8 jit_solution(10626801947152610355)
XLA Ops:
  2.2 2.1 convolution_convert_fusion.3
  5.9 5.9 %all_gather.6 = bf16[64,1024]{1,0:T(8,128)(2,1)S(1)} all-gather(bf16[32,1024]{1,0:T(8,128)(2,1)S(1)} %convolution_convert_fusion.1), channel_id=1, replica_groups=mesh['blk'=16,'quarter'=2] {'quarter'}, dimensions={0}, use_global_device_ids=true | all-gather | bytes 196608 | tf_op jit(solution)/shard_map/all_gather | solution.py:46
  12.7 2.1 convolution_convert_fusion
  14.8 4.9 %all_gather.7 = bf16[64,1024]{1,0:T(8,128)(2,1)S(1)} all-gather(bf16[32,1024]{1,0:T(8,128)(2,1)S(1)} %convolution_convert_fusion), channel_id=1, replica_groups=mesh['blk'=16,'quarter'=2] {'quarter'}, dimensions={0}, use_global_device_ids=true | all-gather | bytes 196608 | tf_op jit(solution)/shard_map/all_gather | solution.py:47
  21.2 269.2 %while.25 = (s32[]{:T(128)}, bf16[32,1024]{1,0:T(8,128)(2,1)}, bf16[32,1024]{1,0:T(8,128)(2,1)}, f32[16,32]{1,0:T(8,128)S(1)}, f32[16,32]{1,0:T(8,128)}, /*index...) while((s32[]{:T(128)}, bf16[32,1024]{1,0:T(8,128)(2,1)}, ...), condition=%wide.region_5.0_spmd.clone, body=%wide.region_0.0_spmd.clone.sunk | while | flops 13213187 | bytes 7352685 | solution.py:112
  22.9 2.1 collective-permute-start.1
  36.9 3.2 %collective-permute-done.4 = f32[32,1024]{1,0:T(8,128)} collective-permute-done((f32[32,1024]{1,0:T(8,128)}, f32[32,1024]{1,0:T(8,128)}, u32[]{:S(2)}, u32[]{:S(2)}) %collective-permute-start.4) | collective-permute-done | bytes 131104 | tf_op jit(solution)/shard_map/while/body/eval_jaxpr/ppermute | solution.py:19
  54.7 2.1 collective-permute-done.4
  67.6 1.7 fusion.55
  71.3 2.0 collective-permute-done.4
  83.5 1.7 fusion.55
  89.3 2.0 collective-permute-start
  101.1 1.7 fusion.55
  104.8 2.1 collective-permute-done.4
  117.7 1.7 fusion.55
  121.4 2.1 collective-permute-done.4
  137.9 2.2 collective-permute-done.4
  155.0 1.8 collective-permute-done.4
  171.6 2.1 collective-permute-done.4
  188.2 2.1 collective-permute-done.4
  205.0 1.9 collective-permute-done.4
  221.8 1.8 collective-permute-done.4
  238.4 2.1 collective-permute-done.4
  255.0 2.1 collective-permute-done.4
  271.7 1.9 collective-permute-done.4
  288.6 1.8 collective-permute-done.4
  291.9 3.2 %all-to-all-start.2 = ((f32[2,1,512]{2,1,0:T(1,128)}), f32[2,1,512]{2,1,0:T(1,128)S(1)}, u32[]{:S(2)}, u32[]{:S(2)}) async-start(f32[2,1,512]{2,1,0:T(1,128)} %reshape.87), calls=%async_computation.2 | async-start | bytes 8192 | tf_op jit(solution)/shard_map/all_to_all | solution.py:136
  298.9 3.2 %all-to-all-start.1 = ((f32[2,1,512]{2,1,0:T(1,128)}), f32[2,1,512]{2,1,0:T(1,128)S(1)}, u32[]{:S(2)}, u32[]{:S(2)}) async-start(f32[2,1,512]{2,1,0:T(1,128)} %reshape.85), calls=%async_computation.1 | async-start | bytes 8192 | tf_op jit(solution)/shard_map/all_to_all | solution.py:135
  302.1 2.7 fusion.15
  306.3 3.4 %all-to-all-start = ((f32[2,32,1024]{2,1,0:T(8,128)}), f32[2,32,1024]{2,1,0:T(8,128)S(1)}, u32[]{:S(2)}, u32[]{:S(2)}) async-start(f32[2,32,1024]{2,1,0:T(8,128)} %bitcast), calls=%async_computation | async-start | bytes 524288 | tf_op jit(solution)/shard_map/all_to_all | solution.py:137
  311.3 3.5 %all-to-all-done = f32[2,32,1024]{2,1,0:T(8,128)S(1)} async-done(((f32[2,32,1024]{2,1,0:T(8,128)}), f32[2,32,1024]{2,1,0:T(8,128)S(1)}, u32[]{:S(2)}, u32[]{:S(2)}) %all-to-all-start) | async-done | bytes 262176 | tf_op jit(solution)/shard_map/all_to_all | solution.py:137
  315.1 2.7 fusion.14
  (642 shorter events, 239.5 us)
Async XLA Ops:
  22.1 14.8 %collective-permute-start = (bf16[32,1024]{1,0:T(8,128)(2,1)S(1)}, bf16[32,1024]{1,0:T(8,128)(2,1)}, u32[]{:S(2)}, u32[]{:S(2)}) collective-permute-start(bf16[32,1024]{1,0:T(8,128)(2,1)S(1)} %copy.99), channel_id=1, source_target_pairs={{0,2},{2,4},{4,6},{6,8},{8,10},{10,12},{12,14},{14,16},{16,18},{18... | collective-permute-start | bytes 196616 | tf_op jit(solution)/shard_map/while/body/eval_jaxpr/ppermute | solution.py:19
  22.9 14.0 %collective-permute-start.1 = (bf16[32,1024]{1,0:T(8,128)(2,1)S(1)}, bf16[32,1024]{1,0:T(8,128)(2,1)}, u32[]{:S(2)}, u32[]{:S(2)}) collective-permute-start(bf16[32,1024]{1,0:T(8,128)(2,1)S(1)} %copy.100), channel_id=1, source_target_pairs={{0,2},{2,4},{4,6},{6,8},{8,10},{10,12},{12,14},{14,16},{16,18},{18... | collective-permute-start | bytes 196616 | tf_op jit(solution)/shard_map/while/body/eval_jaxpr/ppermute | solution.py:19
  41.0 13.7 %collective-permute-start = (bf16[32,1024]{1,0:T(8,128)(2,1)S(1)}, bf16[32,1024]{1,0:T(8,128)(2,1)}, u32[]{:S(2)}, u32[]{:S(2)}) collective-permute-start(bf16[32,1024]{1,0:T(8,128)(2,1)S(1)} %copy.99), channel_id=1, source_target_pairs={{0,2},{2,4},{4,6},{6,8},{8,10},{10,12},{12,14},{14,16},{16,18},{18... | collective-permute-start | bytes 196616 | tf_op jit(solution)/shard_map/while/body/eval_jaxpr/ppermute | solution.py:19
  41.8 12.8 %collective-permute-start.1 = (bf16[32,1024]{1,0:T(8,128)(2,1)S(1)}, bf16[32,1024]{1,0:T(8,128)(2,1)}, u32[]{:S(2)}, u32[]{:S(2)}) collective-permute-start(bf16[32,1024]{1,0:T(8,128)(2,1)S(1)} %copy.100), channel_id=1, source_target_pairs={{0,2},{2,4},{4,6},{6,8},{8,10},{10,12},{12,14},{14,16},{16,18},{18... | collective-permute-start | bytes 196616 | tf_op jit(solution)/shard_map/while/body/eval_jaxpr/ppermute | solution.py:19
  57.6 13.7 %collective-permute-start = (bf16[32,1024]{1,0:T(8,128)(2,1)S(1)}, bf16[32,1024]{1,0:T(8,128)(2,1)}, u32[]{:S(2)}, u32[]{:S(2)}) collective-permute-start(bf16[32,1024]{1,0:T(8,128)(2,1)S(1)} %copy.99), channel_id=1, source_target_pairs={{0,2},{2,4},{4,6},{6,8},{8,10},{10,12},{12,14},{14,16},{16,18},{18... | collective-permute-start | bytes 196616 | tf_op jit(solution)/shard_map/while/body/eval_jaxpr/ppermute | solution.py:19
  58.4 12.9 %collective-permute-start.1 = (bf16[32,1024]{1,0:T(8,128)(2,1)S(1)}, bf16[32,1024]{1,0:T(8,128)(2,1)}, u32[]{:S(2)}, u32[]{:S(2)}) collective-permute-start(bf16[32,1024]{1,0:T(8,128)(2,1)S(1)} %copy.100), channel_id=1, source_target_pairs={{0,2},{2,4},{4,6},{6,8},{8,10},{10,12},{12,14},{14,16},{16,18},{18... | collective-permute-start | bytes 196616 | tf_op jit(solution)/shard_map/while/body/eval_jaxpr/ppermute | solution.py:19
  74.2 13.1 %collective-permute-start = (bf16[32,1024]{1,0:T(8,128)(2,1)S(1)}, bf16[32,1024]{1,0:T(8,128)(2,1)}, u32[]{:S(2)}, u32[]{:S(2)}) collective-permute-start(bf16[32,1024]{1,0:T(8,128)(2,1)S(1)} %copy.99), channel_id=1, source_target_pairs={{0,2},{2,4},{4,6},{6,8},{8,10},{10,12},{12,14},{14,16},{16,18},{18... | collective-permute-start | bytes 196616 | tf_op jit(solution)/shard_map/while/body/eval_jaxpr/ppermute | solution.py:19
  75.0 12.3 %collective-permute-start.1 = (bf16[32,1024]{1,0:T(8,128)(2,1)S(1)}, bf16[32,1024]{1,0:T(8,128)(2,1)}, u32[]{:S(2)}, u32[]{:S(2)}) collective-permute-start(bf16[32,1024]{1,0:T(8,128)(2,1)S(1)} %copy.100), channel_id=1, source_target_pairs={{0,2},{2,4},{4,6},{6,8},{8,10},{10,12},{12,14},{14,16},{16,18},{18... | collective-permute-start | bytes 196616 | tf_op jit(solution)/shard_map/while/body/eval_jaxpr/ppermute | solution.py:19
  89.3 15.5 %collective-permute-start = (bf16[32,1024]{1,0:T(8,128)(2,1)S(1)}, bf16[32,1024]{1,0:T(8,128)(2,1)}, u32[]{:S(2)}, u32[]{:S(2)}) collective-permute-start(bf16[32,1024]{1,0:T(8,128)(2,1)S(1)} %copy.99), channel_id=1, source_target_pairs={{0,2},{2,4},{4,6},{6,8},{8,10},{10,12},{12,14},{14,16},{16,18},{18... | collective-permute-start | bytes 196616 | tf_op jit(solution)/shard_map/while/body/eval_jaxpr/ppermute | solution.py:19
  92.2 12.6 %collective-permute-start.1 = (bf16[32,1024]{1,0:T(8,128)(2,1)S(1)}, bf16[32,1024]{1,0:T(8,128)(2,1)}, u32[]{:S(2)}, u32[]{:S(2)}) collective-permute-start(bf16[32,1024]{1,0:T(8,128)(2,1)S(1)} %copy.100), channel_id=1, source_target_pairs={{0,2},{2,4},{4,6},{6,8},{8,10},{10,12},{12,14},{14,16},{16,18},{18... | collective-permute-start | bytes 196616 | tf_op jit(solution)/shard_map/while/body/eval_jaxpr/ppermute | solution.py:19
  107.8 13.6 %collective-permute-start = (bf16[32,1024]{1,0:T(8,128)(2,1)S(1)}, bf16[32,1024]{1,0:T(8,128)(2,1)}, u32[]{:S(2)}, u32[]{:S(2)}) collective-permute-start(bf16[32,1024]{1,0:T(8,128)(2,1)S(1)} %copy.99), channel_id=1, source_target_pairs={{0,2},{2,4},{4,6},{6,8},{8,10},{10,12},{12,14},{14,16},{16,18},{18... | collective-permute-start | bytes 196616 | tf_op jit(solution)/shard_map/while/body/eval_jaxpr/ppermute | solution.py:19
  108.8 12.6 %collective-permute-start.1 = (bf16[32,1024]{1,0:T(8,128)(2,1)S(1)}, bf16[32,1024]{1,0:T(8,128)(2,1)}, u32[]{:S(2)}, u32[]{:S(2)}) collective-permute-start(bf16[32,1024]{1,0:T(8,128)(2,1)S(1)} %copy.100), channel_id=1, source_target_pairs={{0,2},{2,4},{4,6},{6,8},{8,10},{10,12},{12,14},{14,16},{16,18},{18... | collective-permute-start | bytes 196616 | tf_op jit(solution)/shard_map/while/body/eval_jaxpr/ppermute | solution.py:19
  124.4 13.5 %collective-permute-start = (bf16[32,1024]{1,0:T(8,128)(2,1)S(1)}, bf16[32,1024]{1,0:T(8,128)(2,1)}, u32[]{:S(2)}, u32[]{:S(2)}) collective-permute-start(bf16[32,1024]{1,0:T(8,128)(2,1)S(1)} %copy.99), channel_id=1, source_target_pairs={{0,2},{2,4},{4,6},{6,8},{8,10},{10,12},{12,14},{14,16},{16,18},{18... | collective-permute-start | bytes 196616 | tf_op jit(solution)/shard_map/while/body/eval_jaxpr/ppermute | solution.py:19
  125.4 12.5 %collective-permute-start.1 = (bf16[32,1024]{1,0:T(8,128)(2,1)S(1)}, bf16[32,1024]{1,0:T(8,128)(2,1)}, u32[]{:S(2)}, u32[]{:S(2)}) collective-permute-start(bf16[32,1024]{1,0:T(8,128)(2,1)S(1)} %copy.100), channel_id=1, source_target_pairs={{0,2},{2,4},{4,6},{6,8},{8,10},{10,12},{12,14},{14,16},{16,18},{18... | collective-permute-start | bytes 196616 | tf_op jit(solution)/shard_map/while/body/eval_jaxpr/ppermute | solution.py:19
  140.9 14.1 %collective-permute-start = (bf16[32,1024]{1,0:T(8,128)(2,1)S(1)}, bf16[32,1024]{1,0:T(8,128)(2,1)}, u32[]{:S(2)}, u32[]{:S(2)}) collective-permute-start(bf16[32,1024]{1,0:T(8,128)(2,1)S(1)} %copy.99), channel_id=1, source_target_pairs={{0,2},{2,4},{4,6},{6,8},{8,10},{10,12},{12,14},{14,16},{16,18},{18... | collective-permute-start | bytes 196616 | tf_op jit(solution)/shard_map/while/body/eval_jaxpr/ppermute | solution.py:19
  141.8 13.2 %collective-permute-start.1 = (bf16[32,1024]{1,0:T(8,128)(2,1)S(1)}, bf16[32,1024]{1,0:T(8,128)(2,1)}, u32[]{:S(2)}, u32[]{:S(2)}) collective-permute-start(bf16[32,1024]{1,0:T(8,128)(2,1)S(1)} %copy.100), channel_id=1, source_target_pairs={{0,2},{2,4},{4,6},{6,8},{8,10},{10,12},{12,14},{14,16},{16,18},{18... | collective-permute-start | bytes 196616 | tf_op jit(solution)/shard_map/while/body/eval_jaxpr/ppermute | solution.py:19
  157.7 13.9 %collective-permute-start = (bf16[32,1024]{1,0:T(8,128)(2,1)S(1)}, bf16[32,1024]{1,0:T(8,128)(2,1)}, u32[]{:S(2)}, u32[]{:S(2)}) collective-permute-start(bf16[32,1024]{1,0:T(8,128)(2,1)S(1)} %copy.99), channel_id=1, source_target_pairs={{0,2},{2,4},{4,6},{6,8},{8,10},{10,12},{12,14},{14,16},{16,18},{18... | collective-permute-start | bytes 196616 | tf_op jit(solution)/shard_map/while/body/eval_jaxpr/ppermute | solution.py:19
  159.0 12.6 %collective-permute-start.1 = (bf16[32,1024]{1,0:T(8,128)(2,1)S(1)}, bf16[32,1024]{1,0:T(8,128)(2,1)}, u32[]{:S(2)}, u32[]{:S(2)}) collective-permute-start(bf16[32,1024]{1,0:T(8,128)(2,1)S(1)} %copy.100), channel_id=1, source_target_pairs={{0,2},{2,4},{4,6},{6,8},{8,10},{10,12},{12,14},{14,16},{16,18},{18... | collective-permute-start | bytes 196616 | tf_op jit(solution)/shard_map/while/body/eval_jaxpr/ppermute | solution.py:19
  174.6 13.6 %collective-permute-start = (bf16[32,1024]{1,0:T(8,128)(2,1)S(1)}, bf16[32,1024]{1,0:T(8,128)(2,1)}, u32[]{:S(2)}, u32[]{:S(2)}) collective-permute-start(bf16[32,1024]{1,0:T(8,128)(2,1)S(1)} %copy.99), channel_id=1, source_target_pairs={{0,2},{2,4},{4,6},{6,8},{8,10},{10,12},{12,14},{14,16},{16,18},{18... | collective-permute-start | bytes 196616 | tf_op jit(solution)/shard_map/while/body/eval_jaxpr/ppermute | solution.py:19
  175.6 12.6 %collective-permute-start.1 = (bf16[32,1024]{1,0:T(8,128)(2,1)S(1)}, bf16[32,1024]{1,0:T(8,128)(2,1)}, u32[]{:S(2)}, u32[]{:S(2)}) collective-permute-start(bf16[32,1024]{1,0:T(8,128)(2,1)S(1)} %copy.100), channel_id=1, source_target_pairs={{0,2},{2,4},{4,6},{6,8},{8,10},{10,12},{12,14},{14,16},{16,18},{18... | collective-permute-start | bytes 196616 | tf_op jit(solution)/shard_map/while/body/eval_jaxpr/ppermute | solution.py:19
  191.1 13.8 %collective-permute-start = (bf16[32,1024]{1,0:T(8,128)(2,1)S(1)}, bf16[32,1024]{1,0:T(8,128)(2,1)}, u32[]{:S(2)}, u32[]{:S(2)}) collective-permute-start(bf16[32,1024]{1,0:T(8,128)(2,1)S(1)} %copy.99), channel_id=1, source_target_pairs={{0,2},{2,4},{4,6},{6,8},{8,10},{10,12},{12,14},{14,16},{16,18},{18... | collective-permute-start | bytes 196616 | tf_op jit(solution)/shard_map/while/body/eval_jaxpr/ppermute | solution.py:19
  192.1 12.8 %collective-permute-start.1 = (bf16[32,1024]{1,0:T(8,128)(2,1)S(1)}, bf16[32,1024]{1,0:T(8,128)(2,1)}, u32[]{:S(2)}, u32[]{:S(2)}) collective-permute-start(bf16[32,1024]{1,0:T(8,128)(2,1)S(1)} %copy.100), channel_id=1, source_target_pairs={{0,2},{2,4},{4,6},{6,8},{8,10},{10,12},{12,14},{14,16},{16,18},{18... | collective-permute-start | bytes 196616 | tf_op jit(solution)/shard_map/while/body/eval_jaxpr/ppermute | solution.py:19
  207.7 14.1 %collective-permute-start = (bf16[32,1024]{1,0:T(8,128)(2,1)S(1)}, bf16[32,1024]{1,0:T(8,128)(2,1)}, u32[]{:S(2)}, u32[]{:S(2)}) collective-permute-start(bf16[32,1024]{1,0:T(8,128)(2,1)S(1)} %copy.99), channel_id=1, source_target_pairs={{0,2},{2,4},{4,6},{6,8},{8,10},{10,12},{12,14},{14,16},{16,18},{18... | collective-permute-start | bytes 196616 | tf_op jit(solution)/shard_map/while/body/eval_jaxpr/ppermute | solution.py:19
  208.9 12.9 %collective-permute-start.1 = (bf16[32,1024]{1,0:T(8,128)(2,1)S(1)}, bf16[32,1024]{1,0:T(8,128)(2,1)}, u32[]{:S(2)}, u32[]{:S(2)}) collective-permute-start(bf16[32,1024]{1,0:T(8,128)(2,1)S(1)} %copy.100), channel_id=1, source_target_pairs={{0,2},{2,4},{4,6},{6,8},{8,10},{10,12},{12,14},{14,16},{16,18},{18... | collective-permute-start | bytes 196616 | tf_op jit(solution)/shard_map/while/body/eval_jaxpr/ppermute | solution.py:19
  224.5 13.9 %collective-permute-start = (bf16[32,1024]{1,0:T(8,128)(2,1)S(1)}, bf16[32,1024]{1,0:T(8,128)(2,1)}, u32[]{:S(2)}, u32[]{:S(2)}) collective-permute-start(bf16[32,1024]{1,0:T(8,128)(2,1)S(1)} %copy.99), channel_id=1, source_target_pairs={{0,2},{2,4},{4,6},{6,8},{8,10},{10,12},{12,14},{14,16},{16,18},{18... | collective-permute-start | bytes 196616 | tf_op jit(solution)/shard_map/while/body/eval_jaxpr/ppermute | solution.py:19
  225.8 12.6 %collective-permute-start.1 = (bf16[32,1024]{1,0:T(8,128)(2,1)S(1)}, bf16[32,1024]{1,0:T(8,128)(2,1)}, u32[]{:S(2)}, u32[]{:S(2)}) collective-permute-start(bf16[32,1024]{1,0:T(8,128)(2,1)S(1)} %copy.100), channel_id=1, source_target_pairs={{0,2},{2,4},{4,6},{6,8},{8,10},{10,12},{12,14},{14,16},{16,18},{18... | collective-permute-start | bytes 196616 | tf_op jit(solution)/shard_map/while/body/eval_jaxpr/ppermute | solution.py:19
  241.3 13.6 %collective-permute-start = (bf16[32,1024]{1,0:T(8,128)(2,1)S(1)}, bf16[32,1024]{1,0:T(8,128)(2,1)}, u32[]{:S(2)}, u32[]{:S(2)}) collective-permute-start(bf16[32,1024]{1,0:T(8,128)(2,1)S(1)} %copy.99), channel_id=1, source_target_pairs={{0,2},{2,4},{4,6},{6,8},{8,10},{10,12},{12,14},{14,16},{16,18},{18... | collective-permute-start | bytes 196616 | tf_op jit(solution)/shard_map/while/body/eval_jaxpr/ppermute | solution.py:19
  242.3 12.6 %collective-permute-start.1 = (bf16[32,1024]{1,0:T(8,128)(2,1)S(1)}, bf16[32,1024]{1,0:T(8,128)(2,1)}, u32[]{:S(2)}, u32[]{:S(2)}) collective-permute-start(bf16[32,1024]{1,0:T(8,128)(2,1)S(1)} %copy.100), channel_id=1, source_target_pairs={{0,2},{2,4},{4,6},{6,8},{8,10},{10,12},{12,14},{14,16},{16,18},{18... | collective-permute-start | bytes 196616 | tf_op jit(solution)/shard_map/while/body/eval_jaxpr/ppermute | solution.py:19
  257.9 13.8 %collective-permute-start = (bf16[32,1024]{1,0:T(8,128)(2,1)S(1)}, bf16[32,1024]{1,0:T(8,128)(2,1)}, u32[]{:S(2)}, u32[]{:S(2)}) collective-permute-start(bf16[32,1024]{1,0:T(8,128)(2,1)S(1)} %copy.99), channel_id=1, source_target_pairs={{0,2},{2,4},{4,6},{6,8},{8,10},{10,12},{12,14},{14,16},{16,18},{18... | collective-permute-start | bytes 196616 | tf_op jit(solution)/shard_map/while/body/eval_jaxpr/ppermute | solution.py:19
  258.9 12.8 %collective-permute-start.1 = (bf16[32,1024]{1,0:T(8,128)(2,1)S(1)}, bf16[32,1024]{1,0:T(8,128)(2,1)}, u32[]{:S(2)}, u32[]{:S(2)}) collective-permute-start(bf16[32,1024]{1,0:T(8,128)(2,1)S(1)} %copy.100), channel_id=1, source_target_pairs={{0,2},{2,4},{4,6},{6,8},{8,10},{10,12},{12,14},{14,16},{16,18},{18... | collective-permute-start | bytes 196616 | tf_op jit(solution)/shard_map/while/body/eval_jaxpr/ppermute | solution.py:19
  274.5 14.1 %collective-permute-start = (bf16[32,1024]{1,0:T(8,128)(2,1)S(1)}, bf16[32,1024]{1,0:T(8,128)(2,1)}, u32[]{:S(2)}, u32[]{:S(2)}) collective-permute-start(bf16[32,1024]{1,0:T(8,128)(2,1)S(1)} %copy.99), channel_id=1, source_target_pairs={{0,2},{2,4},{4,6},{6,8},{8,10},{10,12},{12,14},{14,16},{16,18},{18... | collective-permute-start | bytes 196616 | tf_op jit(solution)/shard_map/while/body/eval_jaxpr/ppermute | solution.py:19
  275.7 12.9 %collective-permute-start.1 = (bf16[32,1024]{1,0:T(8,128)(2,1)S(1)}, bf16[32,1024]{1,0:T(8,128)(2,1)}, u32[]{:S(2)}, u32[]{:S(2)}) collective-permute-start(bf16[32,1024]{1,0:T(8,128)(2,1)S(1)} %copy.100), channel_id=1, source_target_pairs={{0,2},{2,4},{4,6},{6,8},{8,10},{10,12},{12,14},{14,16},{16,18},{18... | collective-permute-start | bytes 196616 | tf_op jit(solution)/shard_map/while/body/eval_jaxpr/ppermute | solution.py:19
  (74 other events, 583.4 us)
where the time goes:
time: 323 us; the launch traced here: 318 us
  other arithmetic  109 us (34%)
  local copies, waits for them, and re-layouts  76.2 us (24%)
  starting transfers between devices  42.6 us (13%)
  matrix products  40.3 us (12%)
  waiting for transfers between devices  37.3 us (12%)
  blocking collectives  10.8 us (3%)
    while x96, local copies, waits for them, and re-layouts  38.2 us
    ppermute x80, waiting for transfers between devices, shifted(): return lax.ppermute(x, axis, [(i, (i + by) % peers) for i in range(peers)])  32.8 us
    ppermute x80, starting transfers between devices, shifted(): return lax.ppermute(x, axis, [(i, (i + by) % peers) for i in range(peers)])  32.7 us
    add x16, other arithmetic, visit(): sens_numer * widen(sens_fade.T) + sens_term.reshape(block_rows, model_width)  26.3 us
    add x16, other arithmetic, visit(): vid_numer * widen(vid_fade.T) + vid_term.reshape(tile_rows, model_width)  25 us
    add x16, other arithmetic, visit(): sens_total = sens_total * sens_fade + jnp.sum(sens_weights, axis=1)  21.4 us
    add x16, other arithmetic, visit(): vid_total = vid_total * vid_fade + jnp.sum(vid_weights, axis=2)  20.9 us
    dot_general x16, matrix products, visit(): jnp.einsum('vhd,shd->hvs', tile_ref.reshape(tile_rows, head_count, head_s...  20.5 us
  transfers between devices with their start and end apart: 83, of which 18 were waited for; matrix products, arithmetic and copies ran while one was open for 62% of the time, Pallas kernels for 0%

commit v1 on v0

v1 whole, which is shorter than its diff:
```python
import jax
import jax.numpy as jnp
from jax import lax
from jax.experimental import pallas as pl
from jax.experimental.pallas import tpu as pltpu
from jax.sharding import PartitionSpec as P

H = 16
STREAMS = 2
AXES = ("blk", "quarter")
LOG2E = 1.4426950408889634


def lanes_below(shape, split):
    return lax.broadcasted_iota(jnp.int32, shape, 1) < split


def half_turn(x):
    return pltpu.roll(x, x.shape[-1] // 2, 1)


def project_kernel(
    members,
    panel,
    sensor_ref,
    video_ref,
    sens_ref_hbm,
    vid_ref_hbm,
    sens_val_hbm,
    vid_val_hbm,
    out_ref,
    weights,
    sems,
):
    rows, width = sensor_ref.shape
    half = rows // 2
    pair = out_ref.shape[-1]
    hbm = (sens_ref_hbm, vid_ref_hbm, sens_val_hbm, vid_val_hbm)
    panels = width // panel

    def copy(j, i):
        cols = pl.ds(j * panel, panel)
        return pltpu.make_async_copy(hbm[i].at[:, cols], weights.at[i, :, cols], sems.at[i, j])

    for j in range(panels):
        for i in range(4):
            copy(j, i).start()
    tokens = (sensor_ref[...], video_ref[...])
    low = lanes_below((rows, pair), pair // 2)
    low_half = lanes_below((half, pair), pair // 2)
    for j in range(panels):
        found = []
        for i in range(4):
            copy(j, i).wait()
            found.append(
                jnp.dot(
                    tokens[i % 2],
                    weights[i, :, pl.ds(j * panel, panel)],
                    preferred_element_type=jnp.float32,
                )
            )
        refs, vals = found[:2], found[2:]
        for k in range(panel // pair):
            cols = slice(k * pair, (k + 1) * pair)
            ref = [f[:, cols] for f in refs]
            ref_turned = [half_turn(f) for f in ref]
            val = [f[:, cols] for f in vals]
            val_turned = [half_turn(f) for f in val]
            for odd in range(2):
                head = (j * panel // pair + k) * 2 + odd
                for stream in range(STREAMS):
                    other = 1 - stream
                    mine = (ref_turned if odd else ref)[stream]
                    turned = (ref if odd else ref_turned)[stream]
                    query = jnp.where(low_half, mine[:half], turned[half:])
                    key_value = jnp.where(
                        low,
                        (ref_turned if odd else ref)[other],
                        (val if odd else val_turned)[other],
                    )
                    query = query.astype(out_ref.dtype)
                    key_value = key_value.astype(out_ref.dtype)
                    for member in range(stream, members, STREAMS):
                        out_ref[head, member, :half, :] = query
                        out_ref[head, member, half:, :] = key_value


def project(sensor, video, weights, members):
    rows, width = sensor.shape
    pair = 2 * width // H
    panel = 2 * pair
    panels = width // panel
    vmem = pl.BlockSpec(memory_space=pltpu.VMEM)
    hbm = pl.BlockSpec(memory_space=pltpu.HBM)
    return pl.pallas_call(
        lambda *refs: project_kernel(members, panel, *refs),
        name="project",
        out_shape=jax.ShapeDtypeStruct((H, members, 3 * rows // 2, pair), sensor.dtype),
        in_specs=[vmem] * 2 + [hbm] * 4,
        out_specs=vmem,
        scratch_shapes=[
            pltpu.VMEM((4, width, width), sensor.dtype),
            pltpu.SemaphoreType.DMA((4, panels)),
        ],
        compiler_params=pltpu.CompilerParams(vmem_limit_bytes=20 * 2**20),
        cost_estimate=pl.CostEstimate(
            flops=8 * rows * width * width, bytes_accessed=8 * width * width, transcendentals=0
        ),
    )(sensor, video, *weights)


def attend_kernel(scale, block, query_ref, token_ref, out_ref):
    sources, depth, pair = token_ref.shape
    half = depth // 3
    key_value = token_ref[:, half:, :].reshape(sources * 2 * half, pair)
    per = block // half
    low = lanes_below((block, pair), pair // 2)
    weigh = lanes_below(key_value.shape, pair // 2)
    value = jnp.where(weigh, jnp.ones_like(key_value), key_value)

    def mixed(query):
        scores = lax.dot_general(
            query, key_value, (((1,), (1,)), ((), ())), preferred_element_type=jnp.float32
        )
        top = jnp.max(scores, axis=1, keepdims=True)
        weights = jnp.exp2((scores - top) * (scale * LOG2E)).astype(key_value.dtype)
        return jnp.dot(weights, value, preferred_element_type=jnp.float32)

    for b in range(out_ref.shape[0] // per):
        packed = query_ref[pl.ds(b * per, per), :half, :].reshape(block, pair)
        packed = packed.astype(jnp.float32)
        first = jnp.where(low, packed, 0.0).astype(key_value.dtype)
        second = jnp.where(low, half_turn(packed), 0.0).astype(key_value.dtype)
        a = mixed(first)
        b_ = mixed(second)
        a = half_turn(a) / a
        b_ = b_ / half_turn(b_)
        both = jnp.where(low, a, b_).astype(out_ref.dtype)
        out_ref[pl.ds(b * per, per), :, :] = both.reshape(per, half, pair)


def attend(query, tokens, head_size):
    half = tokens.shape[1] // 3
    pair = tokens.shape[2]
    count = query.shape[0]
    block = min(128, count * half)
    vmem = pl.BlockSpec(memory_space=pltpu.VMEM)
    keys = tokens.shape[0] * 2 * half
    return pl.pallas_call(
        lambda *refs: attend_kernel(head_size ** (-0.5), block, *refs),
        name="attend",
        out_shape=jax.ShapeDtypeStruct((count, half, pair), tokens.dtype),
        in_specs=[vmem] * 2,
        out_specs=vmem,
        compiler_params=pltpu.CompilerParams(vmem_limit_bytes=40 * 2**20),
        cost_estimate=pl.CostEstimate(
            flops=8 * count * half * pair * keys,
            bytes_accessed=2 * tokens.size,
            transcendentals=2 * count * half * keys,
        ),
    )(query, tokens)


def finish_kernel(
    mixed_ref,
    sensor_ref,
    video_ref,
    sens_gain_ref,
    vid_gain_ref,
    sens_out_ref,
    vid_out_ref,
    sensor_next_ref,
    video_next_ref,
):
    heads, _, half, pair = mixed_ref.shape
    low = lanes_below((half, pair), pair // 2)
    streams = (
        (sensor_ref, sens_gain_ref, sens_out_ref, sensor_next_ref),
        (video_ref, vid_gain_ref, vid_out_ref, video_next_ref),
    )
    for s, (token_ref, gain_ref, weight_ref, next_ref) in enumerate(streams):
        upper, lower = [], []
        for head in range(0, heads, 2):
            even = mixed_ref[head, s, :, :].astype(jnp.float32)
            odd = mixed_ref[head + 1, s, :, :].astype(jnp.float32)
            upper.append(jnp.where(low, even, half_turn(odd)))
            lower.append(jnp.where(low, half_turn(even), odd))
        mixed = jnp.concatenate(
            [jnp.concatenate(upper, axis=1), jnp.concatenate(lower, axis=1)], axis=0
        )
        power = jnp.mean(mixed * mixed, axis=-1, keepdims=True)
        normed = (mixed * lax.rsqrt(power + 1e-06) * gain_ref[...]).astype(weight_ref.dtype)
        update = jnp.dot(normed, weight_ref[...], preferred_element_type=jnp.float32)
        next_ref[...] = (token_ref[...].astype(jnp.float32) + update).astype(next_ref.dtype)


def finish(mixed, sensor, video, sens_gain, vid_gain, sens_out, vid_out):
    vmem = pl.BlockSpec(memory_space=pltpu.VMEM)
    rows, width = sensor.shape
    shape = jax.ShapeDtypeStruct(sensor.shape, sensor.dtype)
    return pl.pallas_call(
        finish_kernel,
        name="finish",
        out_shape=(shape, shape),
        in_specs=[vmem] * 7,
        out_specs=(vmem, vmem),
        compiler_params=pltpu.CompilerParams(vmem_limit_bytes=20 * 2**20),
        cost_estimate=pl.CostEstimate(
            flops=4 * rows * width * width, bytes_accessed=4 * width * width, transcendentals=0
        ),
    )(mixed, sensor, video, sens_gain[None], vid_gain[None], sens_out, vid_out)


def local(
    sensor, video, sens_ref, vid_ref, sens_val, vid_val, sens_out, vid_out, sens_gain, vid_gain
):
    devices = lax.axis_size(AXES[0]) * lax.axis_size(AXES[1])
    members = devices // H
    blocks = members // STREAMS
    rows, width = sensor.shape
    half = rows // 2
    pair = 2 * width // H
    sources = devices // blocks
    me = lax.axis_index(AXES)

    sent = project(sensor, video, (sens_ref, vid_ref, sens_val, vid_val), members)
    tokens = lax.all_to_all(
        sent.reshape(devices, 3 * half, pair), AXES, split_axis=0, concat_axis=0, tiled=True
    )
    query = tokens
    if blocks > 1:
        first = (me % members) // STREAMS * sources
        query = lax.dynamic_slice_in_dim(tokens, first, sources, axis=0)
    mixed = attend(query, tokens, width // H)
    if blocks > 1:
        whole = jnp.zeros((devices, half, pair), mixed.dtype)
        mixed = lax.dynamic_update_slice_in_dim(whole, mixed, first, axis=0)
    mixed = lax.all_to_all(mixed, AXES, split_axis=0, concat_axis=0, tiled=True)
    mixed = mixed.reshape(H, members, half, pair)
    if blocks > 1:
        first = me // sources * STREAMS
        mixed = lax.dynamic_slice_in_dim(mixed, first, STREAMS, axis=1)
    return finish(mixed, sensor, video, sens_gain, vid_gain, sens_out, vid_out)


def solution(mesh):
    rows = P(AXES, None)
    return jax.shard_map(
        local,
        mesh=mesh,
        in_specs=(rows, rows) + (P(),) * 8,
        out_specs=(rows, rows),
        check_vma=False,
    )
```

time: 323 us -> 50.8 us (0.16); the launches traced: 318 us -> 50.4 us
  other arithmetic: 109 us -> 0 us
  local copies, waits for them, and re-layouts: 76.2 us -> 8.07 us
  starting transfers between devices: 42.6 us -> 0 us
  matrix products: 40.3 us -> 0 us
  waiting for transfers between devices: 37.3 us -> 0 us
  blocking collectives: 10.8 us -> 31.3 us
  Pallas kernels: 0 us -> 10.3 us
    add x64 -> x0, other arithmetic: 93.6 us -> none  [the longest x16 26.3 us: visit(): sens_numer * widen(sens_fade.T) + sens_term.reshape(block_rows, model_width)]
    dot_general x54 -> x0, matrix products: 40.3 us -> none  [the longest x16 20.5 us: visit(): jnp.einsum('vhd,shd->hvs', tile_ref.reshape(tile_rows, head_count, head_s...]
    while x96 -> x0, local copies, waits for them, and re-layouts: 38.2 us -> none
    ppermute x80 -> x0, waiting for transfers between devices: 32.8 us -> none  [shifted(): return lax.ppermute(x, axis, [(i, (i + by) % peers) for i in range(peers)])]
    ppermute x80 -> x0, starting transfers between devices: 32.7 us -> none  [shifted(): return lax.ppermute(x, axis, [(i, (i + by) % peers) for i in range(peers)])]
    all_to_all x0 -> x2, blocking collectives: none -> 31.3 us  [the longest x1 19.9 us: local(): lax.all_to_all(sent.reshape(devices, 3 * half, pair), AXES, split_axis=0,...]
    reshape x103 -> x0, local copies, waits for them, and re-layouts: 15.9 us -> none  [the longest x35 5.28 us: widen(): return jnp.repeat(factors, head_size, axis=-1)]
    reduce_sum x20 -> x0, other arithmetic: 13.3 us -> none  [the longest x16 12.1 us: visit(): sens_total = sens_total * sens_fade + jnp.sum(sens_weights, axis=1)]
  transfers between devices with their start and end apart: 83 -> 0, of which waited for: 18 -> 0; matrix products, arithmetic and copies ran while one was open for 62% -> 0% of each run, Pallas kernels for 0% -> 0%
where the time goes in v1:
time: 50.8 us; the launch traced here: 50.4 us
  blocking collectives  31.3 us (62%)
  Pallas kernels  10.3 us (20%)
  local copies, waits for them, and re-layouts  8.07 us (16%)
  between operations  0.73 us (1%)
    all_to_all x1, blocking collectives, local(): lax.all_to_all(sent.reshape(devices, 3 * half, pair), AXES, split_axis=0,...  19.9 us
    all_to_all x1, blocking collectives, local(): mixed = lax.all_to_all(mixed, AXES, split_axis=0, concat_axis=0, tiled=True)  11.5 us
    unnamed x24, local copies, waits for them, and re-layouts  8.07 us
    pallas_call x1, Pallas kernels, project(): pl.pallas_call(lambda *refs: project_kernel(members, panel, *refs), name=...  5.67 us
    pallas_call x1, Pallas kernels, attend(): pl.pallas_call(lambda *refs: attend_kernel(head_size ** (-0.5), block, *r...  2.99 us
    pallas_call x1, Pallas kernels, finish(): pl.pallas_call(finish_kernel, name='finish', out_shape=(shape, shape), in...  1.61 us

profile of v1, /device:TPU:0, one launch (start us, length us, event | category | flops | bytes accessed | tf_op | source)
XLA Modules:
  0.0 50.4 jit_solution(16262585377256243114)
XLA Ops:
  0.6 0.0 copy-start
  0.6 1.6 %copy-done = bf16[1024,1024]{1,0:T(8,128)(2,1)S(1)} copy-done((bf16[1024,1024]{1,0:T(8,128)(2,1)S(1)}, bf16[1024,1024]{1,0:T(8,128)(2,1)}, u32[]{:S(2)}) %copy-start) | copy-done | bytes 2097176
  2.2 0.0 copy-start.1
  2.2 1.6 %copy-done.1 = bf16[1024,1024]{1,0:T(8,128)(2,1)S(1)} copy-done((bf16[1024,1024]{1,0:T(8,128)(2,1)S(1)}, bf16[1024,1024]{1,0:T(8,128)(2,1)}, u32[]{:S(2)}) %copy-start.1) | copy-done | bytes 2097176
  3.8 0.0 copy-start.2
  3.8 1.6 %copy-done.2 = bf16[1024,1024]{1,0:T(8,128)(2,1)S(1)} copy-done((bf16[1024,1024]{1,0:T(8,128)(2,1)S(1)}, bf16[1024,1024]{1,0:T(8,128)(2,1)}, u32[]{:S(2)}) %copy-start.2) | copy-done | bytes 2097176
  5.4 0.0 copy-start.3
  5.4 1.6 %copy-done.3 = bf16[1024,1024]{1,0:T(8,128)(2,1)S(1)} copy-done((bf16[1024,1024]{1,0:T(8,128)(2,1)S(1)}, bf16[1024,1024]{1,0:T(8,128)(2,1)}, u32[]{:S(2)}) %copy-start.3) | copy-done | bytes 2097176
  7.0 0.0 copy-start.6
  7.0 0.8 %copy-done.6 = bf16[32,1024]{1,0:T(8,128)(2,1)S(1)} copy-done((bf16[32,1024]{1,0:T(8,128)(2,1)S(1)}, bf16[32,1024]{1,0:T(8,128)(2,1)}, u32[]{:S(2)}) %copy-start.6) | copy-done | bytes 65560
  7.8 0.0 copy-start.8
  7.8 0.8 %copy-done.8 = bf16[32,1024]{1,0:T(8,128)(2,1)S(1)} copy-done((bf16[32,1024]{1,0:T(8,128)(2,1)S(1)}, bf16[32,1024]{1,0:T(8,128)(2,1)}, u32[]{:S(2)}) %copy-start.8) | copy-done | bytes 65560
  8.7 0.0 copy-start.5
  8.7 5.7 %project.1 = bf16[16,2,48,128]{3,2,1,0:T(8,128)(2,1)S(1)} custom-call(bf16[32,1024]{1,0:T(8,128)(2,1)S(1)} %copy-done.6, bf16[32,1024]{1,0:T(8,128)(2,1)S(1)} %copy-done.8, bf16[1024,1024]{1,0:T(8,128)(2,1)S(1)} %copy-done, bf16[1024,1024]{1,0:T(8,128)(2,1)S(1)} %copy-done.1, bf16[1024,1024]{1,0:T(8,128)(2,1)S(1)} %copy-done.2, bf16[1024,1024]{1,0:T(8,128)(2,1)S(1)} %copy-done.3), custom_call_target="tpu_custom_call" | custom-call | flops 268435456 | bytes 8388608 | tf_op jit(solution)/shard_map/project/pallas_call | solution.py:95
  14.4 0.0 copy-start.4
  14.4 0.0 copy-start.7
  14.4 0.0 copy-start.9
  14.4 0.0 copy-start.10
  14.4 0.0 copy-start.11
  14.4 19.9 %all_to_all.10.refs_0_.refs_1_ = bf16[32,48,128]{2,1,0:T(8,128)(2,1)S(1)} all-to-all(bf16[32,48,128]{2,1,0:T(8,128)(2,1)S(1)} %bitcast.4), channel_id=1, replica_groups=mesh['blk'=16,'quarter'=2] {'blk','quarter'}, dimensions={0} | all-to-all | bytes 786432 | tf_op jit(solution)/shard_map/all_to_all | solution.py:227
  34.3 3.0 %attend.1 = bf16[32,16,128]{2,1,0:T(8,128)(2,1)S(1)} custom-call(bf16[32,48,128]{2,1,0:T(8,128)(2,1)S(1)} %all_to_all.10.refs_0_.refs_1_, bf16[32,48,128]{2,1,0:T(8,128)(2,1)S(1)} %all_to_all.10.refs_0_.refs_1_), custom_call_target="tpu_custom_call" | custom-call | flops 536870912 | bytes 393216 | tf_op jit(solution)/shard_map/attend/pallas_call | solution.py:149
  37.3 11.5 %all_to_all.11 = bf16[32,16,128]{2,1,0:T(8,128)(2,1)S(1)} all-to-all(bf16[32,16,128]{2,1,0:T(8,128)(2,1)S(1)} %attend.1), channel_id=1, replica_groups=mesh['blk'=16,'quarter'=2] {'blk','quarter'}, dimensions={0} | all-to-all | bytes 262144 | tf_op jit(solution)/shard_map/all_to_all | solution.py:238
  48.7 0.0 copy-done.5
  48.7 0.0 copy-done.4
  48.7 0.0 copy-done.7
  48.7 0.0 copy-done.9
  48.8 0.0 copy-done.10
  48.8 0.0 copy-done.11
  48.8 1.6 %finish.1 = (bf16[32,1024]{1,0:T(8,128)(2,1)}, bf16[32,1024]{1,0:T(8,128)(2,1)}) custom-call(bf16[16,2,16,128]{3,2,1,0:T(8,128)(2,1)S(1)} %bitcast.5, bf16[32,1024]{1,0:T(8,128)(2,1)S(1)} %copy-done.7, bf16[32,1024]{1,0:T(8,128)(2,1)S(1)} %copy-done.9, f32[1,1024]{1,0:T(1,128)S(1)} %bitcast.6, f32[1,1024]{1,0:T(1,128)S(1)} %bitcast.7, ...), custom_call_target="tpu_custom_call" | custom-call | flops 134217728 | bytes 4194304 | tf_op jit(solution)/shard_map/finish/pallas_call | solution.py:201
Async XLA Ops:
  0.6 1.6 %copy-start = (bf16[1024,1024]{1,0:T(8,128)(2,1)S(1)}, bf16[1024,1024]{1,0:T(8,128)(2,1)}, u32[]{:S(2)}) copy-start(bf16[1024,1024]{1,0:T(8,128)(2,1)} %refs_2_.1) | copy-start | bytes 6291460
  2.2 1.6 %copy-start.1 = (bf16[1024,1024]{1,0:T(8,128)(2,1)S(1)}, bf16[1024,1024]{1,0:T(8,128)(2,1)}, u32[]{:S(2)}) copy-start(bf16[1024,1024]{1,0:T(8,128)(2,1)} %refs_3_.1) | copy-start | bytes 6291460
  3.8 1.6 %copy-start.2 = (bf16[1024,1024]{1,0:T(8,128)(2,1)S(1)}, bf16[1024,1024]{1,0:T(8,128)(2,1)}, u32[]{:S(2)}) copy-start(bf16[1024,1024]{1,0:T(8,128)(2,1)} %refs_4_.1) | copy-start | bytes 6291460
  5.4 1.6 %copy-start.3 = (bf16[1024,1024]{1,0:T(8,128)(2,1)S(1)}, bf16[1024,1024]{1,0:T(8,128)(2,1)}, u32[]{:S(2)}) copy-start(bf16[1024,1024]{1,0:T(8,128)(2,1)} %refs_5_.1) | copy-start | bytes 6291460
  7.0 0.8 %copy-start.6 = (bf16[32,1024]{1,0:T(8,128)(2,1)S(1)}, bf16[32,1024]{1,0:T(8,128)(2,1)}, u32[]{:S(2)}) copy-start(bf16[32,1024]{1,0:T(8,128)(2,1)} %sensor_ref.1) | copy-start | bytes 196612
  7.8 0.8 %copy-start.8 = (bf16[32,1024]{1,0:T(8,128)(2,1)S(1)}, bf16[32,1024]{1,0:T(8,128)(2,1)}, u32[]{:S(2)}) copy-start(bf16[32,1024]{1,0:T(8,128)(2,1)} %video_ref.1) | copy-start | bytes 196612
  8.7 40.1 %copy-start.5 = (bf16[1024,1024]{1,0:T(8,128)(2,1)S(1)}, bf16[1024,1024]{1,0:T(8,128)(2,1)}, u32[]{:S(2)}) copy-start(bf16[1024,1024]{1,0:T(8,128)(2,1)} %vid_out_ref.1) | copy-start | bytes 6291460
  14.4 34.4 %copy-start.4 = (bf16[1024,1024]{1,0:T(8,128)(2,1)S(1)}, bf16[1024,1024]{1,0:T(8,128)(2,1)}, u32[]{:S(2)}) copy-start(bf16[1024,1024]{1,0:T(8,128)(2,1)} %sens_out_ref.1) | copy-start | bytes 6291460
  14.4 34.4 %copy-start.7 = (bf16[32,1024]{1,0:T(8,128)(2,1)S(1)}, bf16[32,1024]{1,0:T(8,128)(2,1)}, u32[]{:S(2)}) copy-start(bf16[32,1024]{1,0:T(8,128)(2,1)} %sensor_ref.1) | copy-start | bytes 196612
  14.4 34.4 %copy-start.9 = (bf16[32,1024]{1,0:T(8,128)(2,1)S(1)}, bf16[32,1024]{1,0:T(8,128)(2,1)}, u32[]{:S(2)}) copy-start(bf16[32,1024]{1,0:T(8,128)(2,1)} %video_ref.1) | copy-start | bytes 196612
  14.4 34.4 %copy-start.10 = (f32[1024]{0:T(1024)S(1)}, f32[1024]{0:T(1024)}, u32[]{:S(2)}) copy-start(f32[1024]{0:T(1024)} %param.18) | copy-start | bytes 12292
  14.4 34.4 %copy-start.11 = (f32[1024]{0:T(1024)S(1)}, f32[1024]{0:T(1024)}, u32[]{:S(2)}) copy-start(f32[1024]{0:T(1024)} %param.19) | copy-start | bytes 12292

commit v2 on v1

--- a/solution.py
+++ b/solution.py
@@ -9,6 +9,7 @@
 STREAMS = 2
 AXES = ("blk", "quarter")
 LOG2E = 1.4426950408889634
+VMEM_BYTES = 16*2**20
 
 
 def lanes_below(shape, split):
@@ -21,92 +22,83 @@
 
 def project_kernel(
     members,
-    panel,
-    sensor_ref,
-    video_ref,
+    sensor_hbm,
+    video_hbm,
     sens_ref_hbm,
     vid_ref_hbm,
     sens_val_hbm,
     vid_val_hbm,
     out_ref,
+    tokens,
     weights,
-    sems,
+    token_sems,
+    weight_sems,
 ):
-    rows, width = sensor_ref.shape
+    _, rows, width = tokens.shape
     half = rows // 2
     pair = out_ref.shape[-1]
-    hbm = (sens_ref_hbm, vid_ref_hbm, sens_val_hbm, vid_val_hbm)
-    panels = width // panel
-
-    def copy(j, i):
-        cols = pl.ds(j * panel, panel)
-        return pltpu.make_async_copy(hbm[i].at[:, cols], weights.at[i, :, cols], sems.at[i, j])
-
-    for j in range(panels):
-        for i in range(4):
-            copy(j, i).start()
-    tokens = (sensor_ref[...], video_ref[...])
+    weight_hbm = (sens_ref_hbm, vid_ref_hbm, sens_val_hbm, vid_val_hbm)
+    token_copies = [
+        pltpu.make_async_copy(source, tokens.at[s], token_sems.at[s])
+        for s, source in enumerate((sensor_hbm, video_hbm))
+    ]
+    weight_copies = [
+        pltpu.make_async_copy(source, weights.at[i], weight_sems.at[i])
+        for i, source in enumerate(weight_hbm)
+    ]
+    for copy in token_copies:
+        copy.start()
+    for copy in weight_copies[:STREAMS]:
+        copy.start()
+    for copy in token_copies:
+        copy.wait()
     low = lanes_below((rows, pair), pair // 2)
     low_half = lanes_below((half, pair), pair // 2)
-    for j in range(panels):
-        found = []
-        for i in range(4):
-            copy(j, i).wait()
-            found.append(
-                jnp.dot(
-                    tokens[i % 2],
-                    weights[i, :, pl.ds(j * panel, panel)],
-                    preferred_element_type=jnp.float32,
-                )
-            )
-        refs, vals = found[:2], found[2:]
-        for k in range(panel // pair):
-            cols = slice(k * pair, (k + 1) * pair)
-            ref = [f[:, cols] for f in refs]
-            ref_turned = [half_turn(f) for f in ref]
-            val = [f[:, cols] for f in vals]
-            val_turned = [half_turn(f) for f in val]
-            for odd in range(2):
-                head = (j * panel // pair + k) * 2 + odd
-                for stream in range(STREAMS):
-                    other = 1 - stream
-                    mine = (ref_turned if odd else ref)[stream]
-                    turned = (ref if odd else ref_turned)[stream]
-                    query = jnp.where(low_half, mine[:half], turned[half:])
-                    key_value = jnp.where(
-                        low,
-                        (ref_turned if odd else ref)[other],
-                        (val if odd else val_turned)[other],
-                    )
-                    query = query.astype(out_ref.dtype)
-                    key_value = key_value.astype(out_ref.dtype)
-                    for member in range(stream, members, STREAMS):
-                        out_ref[head, member, :half, :] = query
-                        out_ref[head, member, half:, :] = key_value
+    keys = {}
+    for i in range(2 * STREAMS):
+        stream = i % STREAMS
+        weight_copies[i].wait()
+        if i < STREAMS:
+            weight_copies[i + STREAMS].start()
+        found = jnp.dot(tokens[stream], weights[i], preferred_element_type=jnp.float32)
+        for head in range(H):
+            first = head // 2 * pair
+            straight = found[:, first : first + pair]
+            turned = half_turn(straight)
+            below, above = (turned, straight) if head % 2 else (straight, turned)
+            if i < STREAMS:
+                query = jnp.where(low_half, below[:half], above[half:]).astype(out_ref.dtype)
+                for member in range(stream, members, STREAMS):
+                    out_ref[head, member, :half, :] = query
+                keys[stream, head] = below.astype(out_ref.dtype)
+            else:
+                key_value = jnp.where(low, keys[stream, head], above.astype(out_ref.dtype))
+                for member in range(1 - stream, members, STREAMS):
+                    out_ref[head, member, half:, :] = key_value
 
 
 def project(sensor, video, weights, members):
+    operands = [pltpu.with_memory_space_constraint(x, pltpu.HBM) for x in (sensor, video) + weights]
     rows, width = sensor.shape
     pair = 2 * width // H
-    panel = 2 * pair
-    panels = width // panel
-    vmem = pl.BlockSpec(memory_space=pltpu.VMEM)
     hbm = pl.BlockSpec(memory_space=pltpu.HBM)
     return pl.pallas_call(
-        lambda *refs: project_kernel(members, panel, *refs),
+        lambda *refs: project_kernel(members, *refs),
         name="project",
         out_shape=jax.ShapeDtypeStruct((H, members, 3 * rows // 2, pair), sensor.dtype),
-        in_specs=[vmem] * 2 + [hbm] * 4,
-        out_specs=vmem,
+        in_specs=[hbm] * 6,
+        out_specs=pl.BlockSpec(memory_space=pltpu.VMEM),
         scratch_shapes=[
-            pltpu.VMEM((4, width, width), sensor.dtype),
-            pltpu.SemaphoreType.DMA((4, panels)),
+            pltpu.VMEM((STREAMS, rows, width), sensor.dtype),
+            pltpu.VMEM((2 * STREAMS, width, width), sensor.dtype),
+            pltpu.SemaphoreType.DMA((STREAMS,)),
+            pltpu.SemaphoreType.DMA((2 * STREAMS,)),
         ],
-        compiler_params=pltpu.CompilerParams(vmem_limit_bytes=20 * 2**20),
+        compiler_params=pltpu.CompilerParams(vmem_limit_bytes=VMEM_BYTES),
         cost_estimate=pl.CostEstimate(
             flops=8 * rows * width * width, bytes_accessed=8 * width * width, transcendentals=0
         ),
-    )(sensor, video, *weights)
+    )(*operands)
 
 
 def attend_kernel(scale, block, query_ref, token_ref, out_ref):
@@ -131,8 +123,8 @@
         packed = packed.astype(jnp.float32)
         first = jnp.where(low, packed, 0.0).astype(key_value.dtype)
         second = jnp.where(low, half_turn(packed), 0.0).astype(key_value.dtype)
-        a = mixed(first)
-        b_ = mixed(second)
+        ab = mixed(jnp.concatenate([first, second], axis=0))
+        a, b_ = ab[:block], ab[block:]
         a = half_turn(a) / a
         b_ = b_ / half_turn(b_)
         both = jnp.where(low, a, b_).astype(out_ref.dtype)
@@ -143,18 +135,20 @@
     half = tokens.shape[1] // 3
     pair = tokens.shape[2]
     count = query.shape[0]
-    block = min(128, count * half)
     vmem = pl.BlockSpec(memory_space=pltpu.VMEM)
     keys = tokens.shape[0] * 2 * half
+    block = count * half
+    while block % (2 * half) == 0 and block * keys > 2**18:
+        block //= 2
     return pl.pallas_call(
         lambda *refs: attend_kernel(head_size ** (-0.5), block, *refs),
         name="attend",
         out_shape=jax.ShapeDtypeStruct((count, half, pair), tokens.dtype),
         in_specs=[vmem] * 2,
         out_specs=vmem,
-        compiler_params=pltpu.CompilerParams(vmem_limit_bytes=40 * 2**20),
+        compiler_params=pltpu.CompilerParams(vmem_limit_bytes=12 * 2**20),
         cost_estimate=pl.CostEstimate(
-            flops=8 * count * half * pair * keys,
+            flops=64 * count * half * pair * keys,
             bytes_accessed=2 * tokens.size,
             transcendentals=2 * count * half * keys,
         ),
@@ -204,7 +198,7 @@
         out_shape=(shape, shape),
         in_specs=[vmem] * 7,
         out_specs=(vmem, vmem),
-        compiler_params=pltpu.CompilerParams(vmem_limit_bytes=20 * 2**20),
+        compiler_params=pltpu.CompilerParams(vmem_limit_bytes=8 * 2**20),
         cost_estimate=pl.CostEstimate(
             flops=4 * rows * width * width, bytes_accessed=4 * width * width, transcendentals=0
         ),

time: 50.8 us -> 40.4 us (0.80)
  local copies, waits for them, and re-layouts: 8.07 us -> 0.03 us
  Pallas kernels: 10.3 us -> 8.2 us
    unnamed x24 -> x12, local copies, waits for them, and re-layouts: 8.07 us -> 0.03 us
    pallas_call x1, Pallas kernels: 5.67 us -> 4.6 us  [project(): pl.pallas_call(lambda *refs: project_kernel(members, *refs), name='projec...]
    pallas_call x1, Pallas kernels: 2.99 us -> 1.99 us  [attend(): pl.pallas_call(lambda *refs: attend_kernel(head_size ** (-0.5), block, *r...]
where the time goes in v2:
time: 40.4 us; the launch traced here: 40.2 us
  blocking collectives  31.3 us (77%)
  Pallas kernels  8.2 us (20%)
  between operations  0.7 us (2%)
    all_to_all x1, blocking collectives, local(): lax.all_to_all(sent.reshape(devices, 3 * half, pair), AXES, split_axis=0,...  19.9 us
    all_to_all x1, blocking collectives, local(): mixed = lax.all_to_all(mixed, AXES, split_axis=0, concat_axis=0, tiled=True)  11.5 us
    pallas_call x1, Pallas kernels, project(): pl.pallas_call(lambda *refs: project_kernel(members, *refs), name='projec...  4.6 us
    pallas_call x1, Pallas kernels, attend(): pl.pallas_call(lambda *refs: attend_kernel(head_size ** (-0.5), block, *r...  1.99 us
    pallas_call x1, Pallas kernels, finish(): pl.pallas_call(finish_kernel, name='finish', out_shape=(shape, shape), in...  1.61 us

profile of v2, /device:TPU:0, one launch (start us, length us, event | category | flops | bytes accessed | tf_op | source)
XLA Modules:
  0.0 40.2 jit_solution(6231232318548681566)
XLA Ops:
  0.6 4.6 %project.1 = bf16[16,2,48,128]{3,2,1,0:T(8,128)(2,1)S(1)} custom-call(bf16[32,1024]{1,0:T(8,128)(2,1)} %sensor_ref.1, bf16[32,1024]{1,0:T(8,128)(2,1)} %video_ref.1, bf16[1024,1024]{1,0:T(8,128)(2,1)} %refs_2_.1, bf16[1024,1024]{1,0:T(8,128)(2,1)} %refs_3_.1, bf16[1024,1024]{1,0:T(8,128)(2,1)} %refs_4_.1, bf16[1024,1024]{1,0:T(8,128)(2,1)} %refs_5_.1), custom_call_target="tpu_custom_call" | custom-call | flops 268435456 | bytes 8388608 | tf_op jit(solution)/shard_map/project/pallas_call | solution.py:85
  5.2 19.9 %all_to_all.10.refs_0_.refs_1_ = bf16[32,48,128]{2,1,0:T(8,128)(2,1)S(1)} all-to-all(bf16[32,48,128]{2,1,0:T(8,128)(2,1)S(1)} %bitcast.4), channel_id=1, replica_groups=mesh['blk'=16,'quarter'=2] {'blk','quarter'}, dimensions={0} | all-to-all | bytes 786432 | tf_op jit(solution)/shard_map/all_to_all | solution.py:221
  25.1 0.0 copy-start
  25.1 0.0 copy-start.1
  25.1 0.0 copy-start.2
  25.1 0.0 copy-start.3
  25.1 0.0 copy-start.4
  25.1 0.0 copy-start.5
  25.1 2.0 %attend.1 = bf16[32,16,128]{2,1,0:T(8,128)(2,1)S(1)} custom-call(bf16[32,48,128]{2,1,0:T(8,128)(2,1)S(1)} %all_to_all.10.refs_0_.refs_1_, bf16[32,48,128]{2,1,0:T(8,128)(2,1)S(1)} %all_to_all.10.refs_0_.refs_1_), custom_call_target="tpu_custom_call" | custom-call | flops 4294967296 | bytes 393216 | tf_op jit(solution)/shard_map/attend/pallas_call | solution.py:143
  27.1 11.5 %all_to_all.11 = bf16[32,16,128]{2,1,0:T(8,128)(2,1)S(1)} all-to-all(bf16[32,16,128]{2,1,0:T(8,128)(2,1)S(1)} %attend.1), channel_id=1, replica_groups=mesh['blk'=16,'quarter'=2] {'blk','quarter'}, dimensions={0} | all-to-all | bytes 262144 | tf_op jit(solution)/shard_map/all_to_all | solution.py:232
  38.6 0.0 copy-done
  38.6 0.0 copy-done.1
  38.6 0.0 copy-done.2
  38.6 0.0 copy-done.3
  38.6 0.0 copy-done.4
  38.6 0.0 copy-done.5
  38.6 1.6 %finish.1 = (bf16[32,1024]{1,0:T(8,128)(2,1)}, bf16[32,1024]{1,0:T(8,128)(2,1)}) custom-call(bf16[16,2,16,128]{3,2,1,0:T(8,128)(2,1)S(1)} %bitcast.5, bf16[32,1024]{1,0:T(8,128)(2,1)S(1)} %copy-done.2, bf16[32,1024]{1,0:T(8,128)(2,1)S(1)} %copy-done.3, f32[1,1024]{1,0:T(1,128)S(1)} %bitcast.6, f32[1,1024]{1,0:T(1,128)S(1)} %bitcast.7, ...), custom_call_target="tpu_custom_call" | custom-call | flops 134217728 | bytes 4194304 | tf_op jit(solution)/shard_map/finish/pallas_call | solution.py:195
Async XLA Ops:
  25.1 13.5 %copy-start = (bf16[1024,1024]{1,0:T(8,128)(2,1)S(1)}, bf16[1024,1024]{1,0:T(8,128)(2,1)}, u32[]{:S(2)}) copy-start(bf16[1024,1024]{1,0:T(8,128)(2,1)} %sens_out_ref.1) | copy-start | bytes 6291460
  25.1 13.5 %copy-start.1 = (bf16[1024,1024]{1,0:T(8,128)(2,1)S(1)}, bf16[1024,1024]{1,0:T(8,128)(2,1)}, u32[]{:S(2)}) copy-start(bf16[1024,1024]{1,0:T(8,128)(2,1)} %vid_out_ref.1) | copy-start | bytes 6291460
  25.1 13.5 %copy-start.2 = (bf16[32,1024]{1,0:T(8,128)(2,1)S(1)}, bf16[32,1024]{1,0:T(8,128)(2,1)}, u32[]{:S(2)}) copy-start(bf16[32,1024]{1,0:T(8,128)(2,1)} %sensor_ref.1) | copy-start | bytes 196612
  25.1 13.5 %copy-start.3 = (bf16[32,1024]{1,0:T(8,128)(2,1)S(1)}, bf16[32,1024]{1,0:T(8,128)(2,1)}, u32[]{:S(2)}) copy-start(bf16[32,1024]{1,0:T(8,128)(2,1)} %video_ref.1) | copy-start | bytes 196612
  25.1 13.5 %copy-start.4 = (f32[1024]{0:T(1024)S(1)}, f32[1024]{0:T(1024)}, u32[]{:S(2)}) copy-start(f32[1024]{0:T(1024)} %param.18) | copy-start | bytes 12292
  25.1 13.5 %copy-start.5 = (f32[1024]{0:T(1024)S(1)}, f32[1024]{0:T(1024)}, u32[]{:S(2)}) copy-start(f32[1024]{0:T(1024)} %param.19) | copy-start | bytes 12292

commit v3 on v2

v3 whole, which is shorter than its diff:
```python
import jax
import jax.numpy as jnp
from jax import lax
from jax.experimental import pallas as pl
from jax.experimental.pallas import tpu as pltpu
from jax.sharding import Mesh
from jax.sharding import PartitionSpec as P

H = 16
STREAMS = 2
ORDER = ("cell", "quarter", "core")
LOG2E = 1.4426950408889634
FLIGHT = 2


def lanes_below(shape, split):
    return lax.broadcasted_iota(jnp.int32, shape, 1) < split


def half_turn(x):
    return pltpu.roll(x, x.shape[-1] // 2, 1)


def project_kernel(
    sensor_hbm,
    video_hbm,
    sens_ref_hbm,
    vid_ref_hbm,
    sens_val_hbm,
    vid_val_hbm,
    out_ref,
    tokens,
    weights,
    token_sems,
    weight_sems,
):
    _, rows, _ = tokens.shape
    heads, blocks, _, _, pair = out_ref.shape
    token_copies = [
        pltpu.make_async_copy(source, tokens.at[s], token_sems.at[s])
        for s, source in enumerate((sensor_hbm, video_hbm))
    ]
    order = ((sens_ref_hbm, 0), (vid_val_hbm, 1), (vid_ref_hbm, 1), (sens_val_hbm, 0))
    weight_copies = [
        pltpu.make_async_copy(source, weights.at[i], weight_sems.at[i])
        for i, (source, _) in enumerate(order)
    ]
    for copy in token_copies:
        copy.start()
    for copy in weight_copies[:FLIGHT]:
        copy.start()
    for copy in token_copies:
        copy.wait()
    low = lanes_below((rows, pair), pair // 2)
    for stream in range(STREAMS):
        found = []
        for i in (2 * stream, 2 * stream + 1):
            weight_copies[i].wait()
            if i + FLIGHT < len(weight_copies):
                weight_copies[i + FLIGHT].start()
            found.append(
                jnp.dot(tokens[order[i][1]], weights[i], preferred_element_type=jnp.float32)
            )
        for head in range(heads):
            first = head // 2 * pair
            ref, val = (f[:, first : first + pair] for f in found)
            if head % 2:
                ref = half_turn(ref)
            else:
                val = half_turn(val)
            both = jnp.where(low, ref, val).astype(out_ref.dtype)
            for block in range(blocks):
                out_ref[head, block, stream, :, :] = both


def project(sensor, video, weights, blocks):
    rows, width = sensor.shape
    pair = 2 * width // H
    hbm = pl.BlockSpec(memory_space=pltpu.HBM)
    operands = [
        pltpu.with_memory_space_constraint(x, pltpu.HBM) for x in (sensor, video) + weights
    ]
    return pl.pallas_call(
        project_kernel,
        name="project",
        out_shape=jax.ShapeDtypeStruct((H, blocks, STREAMS, rows, pair), sensor.dtype),
        in_specs=[hbm] * 6,
        out_specs=pl.BlockSpec(memory_space=pltpu.VMEM),
        scratch_shapes=[
            pltpu.VMEM((STREAMS, rows, width), sensor.dtype),
            pltpu.VMEM((2 * STREAMS, width, width), sensor.dtype),
            pltpu.SemaphoreType.DMA((STREAMS,)),
            pltpu.SemaphoreType.DMA((2 * STREAMS,)),
        ],
        compiler_params=pltpu.CompilerParams(vmem_limit_bytes=16 * 2**20),
        cost_estimate=pl.CostEstimate(
            flops=8 * rows * width * width, bytes_accessed=8 * width * width, transcendentals=0
        ),
    )(*operands)


def attend_kernel(scale, block, query_ref, own_ref, other_ref, out_ref):
    sources, rows, pair = own_ref.shape
    half = rows // 2
    keys = other_ref[...].reshape(sources * rows, pair)
    values = own_ref[...].reshape(sources * rows, pair)
    values = jnp.where(lanes_below(values.shape, pair // 2), jnp.ones_like(values), values)
    per = block // rows
    low = lanes_below((block, pair), pair // 2)
    low_half = lanes_below((block // 2, pair), pair // 2)
    for b in range(out_ref.shape[0] // per):
        query = query_ref[pl.ds(b * per, per), :, :].reshape(block, pair)
        query = jnp.where(low, query, jnp.zeros_like(query))
        scores = lax.dot_general(
            query, keys, (((1,), (1,)), ((), ())), preferred_element_type=jnp.float32
        )
        top = jnp.max(scores, axis=1, keepdims=True)
        weights = jnp.exp2((scores - top) * (scale * LOG2E)).astype(values.dtype)
        mixed = jnp.dot(weights, values, preferred_element_type=jnp.float32)
        mixed = (mixed / half_turn(mixed)).reshape(per, rows, pair)
        first = mixed[:, :half, :].reshape(block // 2, pair)
        second = mixed[:, half:, :].reshape(block // 2, pair)
        both = jnp.where(low_half, half_turn(first), second).astype(out_ref.dtype)
        out_ref[pl.ds(b * per, per), :, :] = both.reshape(per, half, pair)


def attend(query, own, other, head_size):
    sources, rows, pair = own.shape
    count = query.shape[0]
    keys = sources * rows
    block = count * rows
    while block % (2 * rows) == 0 and block * keys > 2**19:
        block //= 2
    vmem = pl.BlockSpec(memory_space=pltpu.VMEM)
    return pl.pallas_call(
        lambda *refs: attend_kernel(head_size ** (-0.5), block, *refs),
        name="attend",
        out_shape=jax.ShapeDtypeStruct((count, rows // 2, pair), own.dtype),
        in_specs=[vmem] * 3,
        out_specs=vmem,
        compiler_params=pltpu.CompilerParams(vmem_limit_bytes=16 * 2**20),
        cost_estimate=pl.CostEstimate(
            flops=32 * count * rows * pair * keys,
            bytes_accessed=4 * own.size,
            transcendentals=count * rows * keys,
        ),
    )(query, own, other)


def finish_kernel(
    mixed_ref,
    sensor_ref,
    video_ref,
    sens_gain_ref,
    vid_gain_ref,
    sens_out_ref,
    vid_out_ref,
    sensor_next_ref,
    video_next_ref,
):
    heads, _, half, pair = mixed_ref.shape
    low = lanes_below((half, pair), pair // 2)
    streams = (
        (sensor_ref, sens_gain_ref, sens_out_ref, sensor_next_ref),
        (video_ref, vid_gain_ref, vid_out_ref, video_next_ref),
    )
    for s, (token_ref, gain_ref, weight_ref, next_ref) in enumerate(streams):
        upper, lower = [], []
        for head in range(0, heads, 2):
            even = mixed_ref[head, s, :, :].astype(jnp.float32)
            odd = mixed_ref[head + 1, s, :, :].astype(jnp.float32)
            upper.append(jnp.where(low, even, half_turn(odd)))
            lower.append(jnp.where(low, half_turn(even), odd))
        mixed = jnp.concatenate(
            [jnp.concatenate(upper, axis=1), jnp.concatenate(lower, axis=1)], axis=0
        )
        power = jnp.mean(mixed * mixed, axis=-1, keepdims=True)
        normed = (mixed * lax.rsqrt(power + 1e-06) * gain_ref[...]).astype(weight_ref.dtype)
        update = jnp.dot(normed, weight_ref[...], preferred_element_type=jnp.float32)
        next_ref[...] = (token_ref[...].astype(jnp.float32) + update).astype(next_ref.dtype)


def finish(mixed, sensor, video, sens_gain, vid_gain, sens_out, vid_out):
    vmem = pl.BlockSpec(memory_space=pltpu.VMEM)
    rows, width = sensor.shape
    shape = jax.ShapeDtypeStruct(sensor.shape, sensor.dtype)
    return pl.pallas_call(
        finish_kernel,
        name="finish",
        out_shape=(shape, shape),
        in_specs=[vmem] * 7,
        out_specs=(vmem, vmem),
        compiler_params=pltpu.CompilerParams(vmem_limit_bytes=8 * 2**20),
        cost_estimate=pl.CostEstimate(
            flops=4 * rows * width * width, bytes_accessed=4 * width * width, transcendentals=0
        ),
    )(mixed, sensor, video, sens_gain[None], vid_gain[None], sens_out, vid_out)


def local(
    sensor, video, sens_ref, vid_ref, sens_val, vid_val, sens_out, vid_out, sens_gain, vid_gain
):
    devices = lax.axis_size(ORDER)
    blocks = devices // (STREAMS * H)
    sources = devices // blocks
    rows, width = sensor.shape
    half = rows // 2
    pair = 2 * width // H
    me = lax.axis_index(ORDER)

    sent = project(sensor, video, (sens_ref, vid_ref, sens_val, vid_val), blocks)
    own = lax.all_to_all(
        sent.reshape(devices, rows, pair), ORDER, split_axis=0, concat_axis=0, tiled=True
    )
    other = lax.ppermute(own, "core", [(0, 1), (1, 0)])
    query = own
    if blocks > 1:
        first = me // STREAMS % blocks * sources
        query = lax.dynamic_slice_in_dim(own, first, sources, axis=0)
    mixed = attend(query, own, other, width // H)
    if blocks > 1:
        whole = jnp.zeros((devices, half, pair), mixed.dtype)
        mixed = lax.dynamic_update_slice_in_dim(whole, mixed, first, axis=0)
    mixed = lax.all_to_all(mixed, ORDER, split_axis=0, concat_axis=0, tiled=True)
    mixed = mixed.reshape(H, blocks * STREAMS, half, pair)
    if blocks > 1:
        mixed = lax.dynamic_slice_in_dim(mixed, me // sources * STREAMS, STREAMS, axis=1)
    return finish(mixed, sensor, video, sens_gain, vid_gain, sens_out, vid_out)


def solution(mesh):
    cells, quarters = mesh.devices.shape[0] // STREAMS, mesh.devices.shape[1]
    split = Mesh(mesh.devices.reshape(cells, STREAMS, quarters), ("cell", "core", "quarter"))
    rows = P(("cell", "core", "quarter"), None)
    return jax.shard_map(
        local,
        mesh=split,
        in_specs=(rows, rows) + (P(),) * 8,
        out_specs=(rows, rows),
        check_vma=False,
    )
```

time: 40.4 us -> 38.8 us (0.960)
  blocking collectives: 31.3 us -> 28.1 us
  waiting for transfers between devices: 0 us -> 1.52 us
    all_to_all x2, blocking collectives: 31.3 us -> 28.1 us  [the longest x1 17.7 us: local(): lax.all_to_all(sent.reshape(devices, rows, pair), ORDER, split_axis=0, co...]
    ppermute x0 -> x1, waiting for transfers between devices: none -> 1.52 us  [local(): other = lax.ppermute(own, 'core', [(0, 1), (1, 0)])]
  transfers between devices with their start and end apart: 0 -> 1, of which waited for: 0 -> 1; matrix products, arithmetic and copies ran while one was open for 0% -> 0% of each run, Pallas kernels for 0% -> 0%
where the time goes in v3:
time: 38.8 us; the launch traced here: 38.6 us
  blocking collectives  28.1 us (72%)
  Pallas kernels  8.21 us (21%)
  waiting for transfers between devices  1.52 us (4%)
  between operations  0.7 us (2%)
    all_to_all x1, blocking collectives, local(): lax.all_to_all(sent.reshape(devices, rows, pair), ORDER, split_axis=0, co...  17.7 us
    all_to_all x1, blocking collectives, local(): lax.all_to_all(mixed, ORDER, split_axis=0, concat_axis=0, tiled=True)  10.4 us
    pallas_call x1, Pallas kernels, project(): pl.pallas_call(project_kernel, name='project', out_shape=jax.ShapeDtypeSt...  4.6 us
    pallas_call x1, Pallas kernels, attend(): pl.pallas_call(lambda *refs: attend_kernel(head_size ** (-0.5), block, *r...  2 us
    pallas_call x1, Pallas kernels, finish(): pl.pallas_call(finish_kernel, name='finish', out_shape=(shape, shape), in...  1.61 us
    ppermute x1, waiting for transfers between devices, local(): other = lax.ppermute(own, 'core', [(0, 1), (1, 0)])  1.52 us
  transfers between devices with their start and end apart: 1, of which 1 were waited for; matrix products, arithmetic and copies ran while one was open for 0% of the time, Pallas kernels for 0%

profile of v3, /device:TPU:0, one launch (start us, length us, event | category | flops | bytes accessed | tf_op | source)
XLA Modules:
  0.0 38.6 jit_solution(1791949076686161638)
XLA Ops:
  0.6 4.6 %project.1 = bf16[16,1,2,32,128]{4,3,2,1,0:T(8,128)(2,1)S(1)} custom-call(bf16[32,1024]{1,0:T(8,128)(2,1)} %sensor_ref.1, bf16[32,1024]{1,0:T(8,128)(2,1)} %video_ref.1, bf16[1024,1024]{1,0:T(8,128)(2,1)} %sens_ref_hbm.1, bf16[1024,1024]{1,0:T(8,128)(2,1)} %vid_ref_hbm.1, bf16[1024,1024]{1,0:T(8,128)(2,1)} %sens_val_hbm.1, bf16[1024,1024]{1,0:T(8,128)(2,1)} %vid_val_hbm.1), custom_call_target="tpu_custom_call" | custom-call | flops 268435456 | bytes 8388608 | tf_op jit(solution)/shard_map/project/pallas_call | solution.py:83
  5.2 17.7 %all_to_all.10.refs_0_.refs_1_ = bf16[32,32,128]{2,1,0:T(8,128)(2,1)S(1)} all-to-all(bf16[32,32,128]{2,1,0:T(8,128)(2,1)S(1)} %bitcast.4), channel_id=1, replica_groups=mesh['cell'=8,'core'=2,'quarter'=2] {'cell','quarter','core'}, dimensions={0} | all-to-all | bytes 524288 | tf_op jit(solution)/shard_map/all_to_all | solution.py:212
  22.9 0.0 copy-start
  22.9 0.0 copy-start.1
  22.9 0.0 copy-start.2
  22.9 0.0 copy-start.3
  23.0 0.0 copy-start.4
  23.0 0.0 copy-start.5
  23.0 0.1 collective-permute-start
  23.1 1.5 %collective-permute-done.refs_2_ = bf16[32,32,128]{2,1,0:T(8,128)(2,1)S(1)} collective-permute-done((bf16[32,32,128]{2,1,0:T(8,128)(2,1)S(1)}, bf16[32,32,128]{2,1,0:T(8,128)(2,1)S(1)}, u32[]{:S(2)}, u32[]{:S(2)}) %collective-permute-start) | collective-permute-done | bytes 262176 | tf_op jit(solution)/shard_map/ppermute | solution.py:215
  24.6 2.0 %attend.1 = bf16[32,16,128]{2,1,0:T(8,128)(2,1)S(1)} custom-call(bf16[32,32,128]{2,1,0:T(8,128)(2,1)S(1)} %all_to_all.10.refs_0_.refs_1_, bf16[32,32,128]{2,1,0:T(8,128)(2,1)S(1)} %all_to_all.10.refs_0_.refs_1_, bf16[32,32,128]{2,1,0:T(8,128)(2,1)S(1)} %collective-permute-done.refs_2_), custom_call_target="tpu_custom_call" | custom-call | flops 4294967296 | bytes 524288 | tf_op jit(solution)/shard_map/attend/pallas_call | solution.py:135
  26.6 10.4 %all_to_all.11 = bf16[32,16,128]{2,1,0:T(8,128)(2,1)S(1)} all-to-all(bf16[32,16,128]{2,1,0:T(8,128)(2,1)S(1)} %attend.1), channel_id=1, replica_groups=mesh['cell'=8,'core'=2,'quarter'=2] {'cell','quarter','core'}, dimensions={0} | all-to-all | bytes 262144 | tf_op jit(solution)/shard_map/all_to_all | solution.py:224
  37.0 0.0 copy-done
  37.0 0.0 copy-done.1
  37.0 0.0 copy-done.2
  37.0 0.0 copy-done.3
  37.0 0.0 copy-done.4
  37.0 0.0 copy-done.5
  37.0 1.6 %finish.1 = (bf16[32,1024]{1,0:T(8,128)(2,1)}, bf16[32,1024]{1,0:T(8,128)(2,1)}) custom-call(bf16[16,2,16,128]{3,2,1,0:T(8,128)(2,1)S(1)} %bitcast.5, bf16[32,1024]{1,0:T(8,128)(2,1)S(1)} %copy-done.2, bf16[32,1024]{1,0:T(8,128)(2,1)S(1)} %copy-done.3, f32[1,1024]{1,0:T(1,128)S(1)} %bitcast.6, f32[1,1024]{1,0:T(1,128)S(1)} %bitcast.7, ...), custom_call_target="tpu_custom_call" | custom-call | flops 134217728 | bytes 4194304 | tf_op jit(solution)/shard_map/finish/pallas_call | solution.py:187
Async XLA Ops:
  22.9 14.0 %copy-start = (bf16[1024,1024]{1,0:T(8,128)(2,1)S(1)}, bf16[1024,1024]{1,0:T(8,128)(2,1)}, u32[]{:S(2)}) copy-start(bf16[1024,1024]{1,0:T(8,128)(2,1)} %sens_out_ref.1) | copy-start | bytes 6291460
  22.9 14.0 %copy-start.1 = (bf16[1024,1024]{1,0:T(8,128)(2,1)S(1)}, bf16[1024,1024]{1,0:T(8,128)(2,1)}, u32[]{:S(2)}) copy-start(bf16[1024,1024]{1,0:T(8,128)(2,1)} %vid_out_ref.1) | copy-start | bytes 6291460
  22.9 14.0 %copy-start.2 = (bf16[32,1024]{1,0:T(8,128)(2,1)S(1)}, bf16[32,1024]{1,0:T(8,128)(2,1)}, u32[]{:S(2)}) copy-start(bf16[32,1024]{1,0:T(8,128)(2,1)} %sensor_ref.1) | copy-start | bytes 196612
  22.9 14.1 %copy-start.3 = (bf16[32,1024]{1,0:T(8,128)(2,1)S(1)}, bf16[32,1024]{1,0:T(8,128)(2,1)}, u32[]{:S(2)}) copy-start(bf16[32,1024]{1,0:T(8,128)(2,1)} %video_ref.1) | copy-start | bytes 196612
  23.0 14.1 %copy-start.4 = (f32[1024]{0:T(1024)S(1)}, f32[1024]{0:T(1024)}, u32[]{:S(2)}) copy-start(f32[1024]{0:T(1024)} %param.18) | copy-start | bytes 12292
  23.0 14.1 %copy-start.5 = (f32[1024]{0:T(1024)S(1)}, f32[1024]{0:T(1024)}, u32[]{:S(2)}) copy-start(f32[1024]{0:T(1024)} %param.19) | copy-start | bytes 12292
  23.0 1.6 %collective-permute-start = (bf16[32,32,128]{2,1,0:T(8,128)(2,1)S(1)}, bf16[32,32,128]{2,1,0:T(8,128)(2,1)S(1)}, u32[]{:S(2)}, u32[]{:S(2)}) collective-permute-start(bf16[32,32,128]{2,1,0:T(8,128)(2,1)S(1)} %all_to_all.10.refs_0_.refs_1_), channel_id=1, source_target_pairs={{0,2},{2,0},{1,3},{3,1},{4,6},{6,4},{5,7},{7,5},{8,10},{10,8},{9,1... | collective-permute-start | bytes 786440 | tf_op jit(solution)/shard_map/ppermute | solution.py:215

commit v4 on v3

v4 whole, which is shorter than its diff:
```python
import jax
import jax.numpy as jnp
from jax import lax
from jax.experimental import pallas as pl
from jax.experimental.pallas import tpu as pltpu
from jax.sharding import Mesh
from jax.sharding import PartitionSpec as P

H = 16
STREAMS = 2
ORDER = ("cell", "quarter", "core")
LOG2E = 1.4426950408889634


def lanes_below(shape, split):
    return lax.broadcasted_iota(jnp.int32, shape, 1) < split


def half_turn(x):
    return pltpu.roll(x, x.shape[-1] // 2, 1)


def fetch_kernel(sens_ref_hbm, sens_val_hbm, vid_ref_hbm, vid_val_hbm, out_ref, sems):
    core = lax.axis_index("core")
    for stream, pair in enumerate(((sens_ref_hbm, sens_val_hbm), (vid_ref_hbm, vid_val_hbm))):

        @pl.when(core == stream)
        def _():
            copies = [
                pltpu.make_async_copy(source, out_ref.at[i], sems.at[i])
                for i, source in enumerate(pair)
            ]
            for copy in copies:
                copy.start()
            for copy in copies:
                copy.wait()


def fetch(sens_ref, sens_val, vid_ref, vid_val):
    hbm = pl.BlockSpec(memory_space=pltpu.HBM)
    operands = [
        pltpu.with_memory_space_constraint(x, pltpu.HBM)
        for x in (sens_ref, sens_val, vid_ref, vid_val)
    ]
    return pl.pallas_call(
        fetch_kernel,
        name="fetch",
        out_shape=jax.ShapeDtypeStruct((2,) + sens_ref.shape, sens_ref.dtype),
        in_specs=[hbm] * 4,
        out_specs=pl.BlockSpec(memory_space=pltpu.VMEM),
        scratch_shapes=[pltpu.SemaphoreType.DMA((2,))],
        compiler_params=pltpu.CompilerParams(vmem_limit_bytes=8 * 2**20),
        cost_estimate=pl.CostEstimate(
            flops=2**30, bytes_accessed=8 * sens_ref.size, transcendentals=0
        ),
    )(*operands)


def project_kernel(
    sensor_ref, video_ref, other_sensor_ref, other_video_ref, weight_ref, out_ref
):
    heads, blocks, halves, rows, pair = out_ref.shape
    half = rows // 2
    sensor_core = lax.axis_index("core") == 0
    first = jnp.where(sensor_core, sensor_ref[...], other_video_ref[...])
    second = jnp.where(sensor_core, other_sensor_ref[...], video_ref[...])
    tokens = jnp.concatenate([first[:half], second[:half], first[half:], second[half:]], axis=0)
    found = [
        jnp.dot(tokens, weight_ref[i], preferred_element_type=jnp.float32) for i in range(2)
    ]
    low = lanes_below((halves * rows, pair), pair // 2)
    for head in range(heads):
        start = head // 2 * pair
        ref, val = (f[:, start : start + pair] for f in found)
        if head % 2:
            ref = half_turn(ref)
        else:
            val = half_turn(val)
        both = jnp.where(low, ref, val).astype(out_ref.dtype)
        for block in range(blocks):
            for part in range(halves):
                out_ref[head, block, part, :, :] = both[part * rows : (part + 1) * rows]


def project(sensor, video, other_sensor, other_video, weights, blocks):
    rows, width = sensor.shape
    pair = 2 * width // H
    vmem = pl.BlockSpec(memory_space=pltpu.VMEM)
    return pl.pallas_call(
        project_kernel,
        name="project",
        out_shape=jax.ShapeDtypeStruct((H, blocks, 2, rows, pair), sensor.dtype),
        in_specs=[vmem] * 5,
        out_specs=vmem,
        compiler_params=pltpu.CompilerParams(vmem_limit_bytes=8 * 2**20),
        cost_estimate=pl.CostEstimate(
            flops=8 * rows * width * width, bytes_accessed=4 * width * width, transcendentals=0
        ),
    )(sensor, video, other_sensor, other_video, weights)


def blocks_of(rows, keys):
    block = rows
    while block % 64 == 0 and block * keys > 2**18:
        block //= 2
    return block


def scored(query, keys):
    low = lanes_below(query.shape, query.shape[-1] // 2)
    query = jnp.where(low, query, jnp.zeros_like(query))
    return lax.dot_general(
        query, keys, (((1,), (1,)), ((), ())), preferred_element_type=jnp.float32
    )


def valued(both):
    low = lanes_below(both.shape, both.shape[-1] // 2)
    return jnp.where(low, jnp.ones_like(both), both)


def stream_rows(ref, stream):
    chips, _, rows, pair = ref.shape
    return ref[:, stream, :, :].reshape(chips * rows, pair)


def attend_near_kernel(factor, query_ref, near_ref, mixed_ref, top_ref):
    rows = query_ref.shape[2]
    for stream in range(STREAMS):
        both = stream_rows(near_ref, 1 - stream)
        values = valued(both)
        count = mixed_ref.shape[1]
        block = blocks_of(count, both.shape[0])
        for start in range(0, count, block):
            chips = slice(start // rows, (start + block) // rows)
            query = query_ref[chips, stream, :, :].reshape(block, both.shape[1])
            scores = scored(query, both)
            top = jnp.max(scores, axis=1, keepdims=True)
            weights = jnp.exp2((scores - top) * factor).astype(both.dtype)
            part = slice(start, start + block)
            mixed_ref[stream, part, :] = jnp.dot(
                weights, values, preferred_element_type=jnp.float32
            )
            top_ref[stream, part, :] = jnp.broadcast_to(top, (block, both.shape[1]))


def attend_far_kernel(factor, query_ref, far_ref, mixed_ref, top_ref, out_ref):
    rows, pair = query_ref.shape[2:]
    half = rows // 2
    count = mixed_ref.shape[1]
    block = blocks_of(count, far_ref.shape[0] * rows)
    boths = [stream_rows(far_ref, 1 - stream) for stream in range(STREAMS)]
    values = [valued(both) for both in boths]
    low = lanes_below((block, pair), pair // 2)
    for start in range(0, count, block):
        chips = slice(start // rows, (start + block) // rows)
        part = slice(start, start + block)
        ends = []
        for stream in range(STREAMS):
            query = query_ref[chips, stream, :, :].reshape(block, pair)
            scores = scored(query, boths[stream])
            near_top = top_ref[stream, part, :]
            top = jnp.maximum(near_top[:, :1], jnp.max(scores, axis=1, keepdims=True))
            weights = jnp.exp2((scores - top) * factor).astype(out_ref.dtype)
            mixed = mixed_ref[stream, part, :] * jnp.exp2((near_top - top) * factor)
            mixed = mixed + jnp.dot(
                weights, values[stream], preferred_element_type=jnp.float32
            )
            if stream == 0:
                ends.append(half_turn(mixed) / mixed)
            else:
                ends.append(mixed / half_turn(mixed))
        both = jnp.where(low, ends[0], ends[1]).astype(out_ref.dtype)
        devices = slice(start // half, (start + block) // half)
        out_ref[devices, :, :] = both.reshape(block // half, half, pair)


def attend_cost(query, tokens):
    chips, _, rows, pair = tokens.shape
    pairs = STREAMS * query.shape[0] * rows * chips * rows
    return pl.CostEstimate(
        flops=32 * pairs * pair, bytes_accessed=4 * tokens.size, transcendentals=pairs
    )


def attend_near(query, near, factor):
    chips, _, rows, pair = query.shape
    vmem = pl.BlockSpec(memory_space=pltpu.VMEM)
    shape = jax.ShapeDtypeStruct((STREAMS, chips * rows, pair), jnp.float32)
    return pl.pallas_call(
        lambda *refs: attend_near_kernel(factor, *refs),
        name="attend_near",
        out_shape=(shape, shape),
        in_specs=[vmem] * 2,
        out_specs=(vmem, vmem),
        compiler_params=pltpu.CompilerParams(vmem_limit_bytes=16 * 2**20),
        cost_estimate=attend_cost(query, near),
    )(query, near)


def attend_far(query, far, mixed, top, factor):
    chips, _, rows, pair = query.shape
    vmem = pl.BlockSpec(memory_space=pltpu.VMEM)
    return pl.pallas_call(
        lambda *refs: attend_far_kernel(factor, *refs),
        name="attend_far",
        out_shape=jax.ShapeDtypeStruct((2 * chips, rows // 2, pair), query.dtype),
        in_specs=[vmem] * 4,
        out_specs=vmem,
        compiler_params=pltpu.CompilerParams(vmem_limit_bytes=16 * 2**20),
        cost_estimate=attend_cost(query, far),
    )(query, far, mixed, top)


def finish_kernel(
    mixed_ref,
    sensor_ref,
    video_ref,
    sens_gain_ref,
    vid_gain_ref,
    sens_out_ref,
    vid_out_ref,
    sensor_next_ref,
    video_next_ref,
):
    heads, halves, half, pair = mixed_ref.shape
    low = lanes_below((half, pair), pair // 2)
    sides = ([[] for _ in range(halves)], [[] for _ in range(halves)])
    for part in range(halves):
        for head in range(0, heads, 2):
            even = mixed_ref[head, part, :, :].astype(jnp.float32)
            odd = mixed_ref[head + 1, part, :, :].astype(jnp.float32)
            sides[0][part].append(jnp.where(low, even, half_turn(odd)))
            sides[1][part].append(jnp.where(low, half_turn(even), odd))
    streams = (
        (sensor_ref, sens_gain_ref, sens_out_ref, sensor_next_ref),
        (video_ref, vid_gain_ref, vid_out_ref, video_next_ref),
    )
    for side, (token_ref, gain_ref, weight_ref, next_ref) in zip(sides, streams):
        mixed = jnp.concatenate([jnp.concatenate(part, axis=1) for part in side], axis=0)
        power = jnp.mean(mixed * mixed, axis=-1, keepdims=True)
        normed = (mixed * lax.rsqrt(power + 1e-06) * gain_ref[...]).astype(weight_ref.dtype)
        update = jnp.dot(normed, weight_ref[...], preferred_element_type=jnp.float32)
        next_ref[...] = (token_ref[...].astype(jnp.float32) + update).astype(next_ref.dtype)


def finish(mixed, sensor, video, sens_gain, vid_gain, sens_out, vid_out):
    vmem = pl.BlockSpec(memory_space=pltpu.VMEM)
    rows, width = sensor.shape
    shape = jax.ShapeDtypeStruct(sensor.shape, sensor.dtype)
    return pl.pallas_call(
        finish_kernel,
        name="finish",
        out_shape=(shape, shape),
        in_specs=[vmem] * 7,
        out_specs=(vmem, vmem),
        compiler_params=pltpu.CompilerParams(vmem_limit_bytes=8 * 2**20),
        cost_estimate=pl.CostEstimate(
            flops=4 * rows * width * width, bytes_accessed=4 * width * width, transcendentals=0
        ),
    )(mixed, sensor, video, sens_gain[None], vid_gain[None], sens_out, vid_out)


def local(
    sensor, video, sens_ref, vid_ref, sens_val, vid_val, sens_out, vid_out, sens_gain, vid_gain
):
    devices = lax.axis_size(ORDER)
    blocks = devices // (STREAMS * H)
    sources = devices // blocks
    rows, width = sensor.shape
    half = rows // 2
    pair = 2 * width // H
    me = lax.axis_index(ORDER)

    chips = sources // 2
    factor = (width // H) ** (-0.5) * LOG2E
    swap = [(0, 1), (1, 0)]

    others = [lax.ppermute(x, "core", swap) for x in (sensor, video)]
    weights = fetch(sens_ref, sens_val, vid_ref, vid_val)
    sent = project(sensor, video, *others, weights, blocks)
    near = lax.all_to_all(
        sent.reshape(devices, rows, pair), ORDER, split_axis=0, concat_axis=0, tiled=True
    )
    far = lax.ppermute(near, "core", swap)
    near = near.reshape(devices // 2, STREAMS, rows, pair)
    far = far.reshape(devices // 2, STREAMS, rows, pair)
    query = near
    if blocks > 1:
        first = me // 2 % blocks * chips
        query = lax.dynamic_slice_in_dim(near, first, chips, axis=0)
    mixed = attend_far(query, far, *attend_near(query, near, factor), factor)
    if blocks > 1:
        whole = jnp.zeros((devices, half, pair), mixed.dtype)
        mixed = lax.dynamic_update_slice_in_dim(whole, mixed, 2 * first, axis=0)
    mixed = lax.all_to_all(mixed, ORDER, split_axis=0, concat_axis=0, tiled=True)
    mixed = mixed.reshape(H, 2 * blocks, half, pair)
    if blocks > 1:
        mixed = lax.dynamic_slice_in_dim(mixed, me // sources * 2, 2, axis=1)
    return finish(mixed, sensor, video, sens_gain, vid_gain, sens_out, vid_out)


def solution(mesh):
    cells, quarters = mesh.devices.shape[0] // STREAMS, mesh.devices.shape[1]
    split = Mesh(mesh.devices.reshape(cells, STREAMS, quarters), ("cell", "core", "quarter"))
    rows = P(("cell", "core", "quarter"), None)
    return jax.shard_map(
        local,
        mesh=split,
        in_specs=(rows, rows) + (P(),) * 8,
        out_specs=(rows, rows),
        check_vma=False,
    )
```

time: 38.8 us -> 37.6 us (0.969)
  waiting for transfers between devices: 1.52 us -> 0.49 us
  Pallas kernels: 8.21 us -> 7.44 us
  starting transfers between devices: 0.07 us -> 0.64 us
    pallas_call x1, Pallas kernels: 4.6 us -> 0.92 us  [project(): pl.pallas_call(project_kernel, name='project', out_shape=jax.ShapeDtypeSt...]
    pallas_call x1 -> x3, Pallas kernels: 2 us -> 4.91 us  [the longest x1 2.24 us: fetch(): pl.pallas_call(fetch_kernel, name='fetch', out_shape=jax.ShapeDtypeStruct...]
    ppermute x1 -> x3, waiting for transfers between devices: 1.52 us -> 0.49 us  [the longest x1 0.49 us: local(): far = lax.ppermute(near, 'core', swap)]
    ppermute x1 -> x3, starting transfers between devices: 0.07 us -> 0.64 us  [the longest x2 0.64 us: local(): others = [lax.ppermute(x, 'core', swap) for x in (sensor, video)]]
  transfers between devices with their start and end apart: 1 -> 3, of which waited for: 1 -> 1; matrix products, arithmetic and copies ran while one was open for 0% -> 0% of each run, Pallas kernels for 0% -> 9%
where the time goes in v4:
time: 37.6 us; the launch traced here: 37.4 us
  blocking collectives  28.1 us (75%)
  Pallas kernels  7.44 us (20%)
  between operations  0.73 us (2%)
  starting transfers between devices  0.64 us (2%)
  waiting for transfers between devices  0.49 us (1%)
    all_to_all x1, blocking collectives, local(): lax.all_to_all(sent.reshape(devices, rows, pair), ORDER, split_axis=0, co...  17.6 us
    all_to_all x1, blocking collectives, local(): lax.all_to_all(mixed, ORDER, split_axis=0, concat_axis=0, tiled=True)  10.4 us
    pallas_call x1, Pallas kernels, fetch(): pl.pallas_call(fetch_kernel, name='fetch', out_shape=jax.ShapeDtypeStruct...  2.24 us
    pallas_call x1, Pallas kernels, attend_far(): pl.pallas_call(lambda *refs: attend_far_kernel(factor, *refs), name='atte...  1.63 us
    pallas_call x1, Pallas kernels, finish(): pl.pallas_call(finish_kernel, name='finish', out_shape=(shape, shape), in...  1.61 us
    pallas_call x1, Pallas kernels, attend_near(): pl.pallas_call(lambda *refs: attend_near_kernel(factor, *refs), name='att...  1.04 us
    pallas_call x1, Pallas kernels, project(): pl.pallas_call(project_kernel, name='project', out_shape=jax.ShapeDtypeSt...  0.92 us
  transfers between devices with their start and end apart: 3, of which 1 were waited for; matrix products, arithmetic and copies ran while one was open for 0% of the time, Pallas kernels for 9%

profile of v4, /device:TPU:0, one launch (start us, length us, event | category | flops | bytes accessed | tf_op | source)
XLA Modules:
  0.0 37.4 jit_solution(13736815359729053307)
XLA Ops:
  0.6 0.0 copy-start.2
  0.6 0.0 copy-start.3
  0.7 0.6 %collective-permute-start = (bf16[32,1024]{1,0:T(8,128)(2,1)}, bf16[32,1024]{1,0:T(8,128)(2,1)S(1)}, u32[]{:S(2)}, u32[]{:S(2)}) collective-permute-start(bf16[32,1024]{1,0:T(8,128)(2,1)} %sensor_ref.3), channel_id=1, source_target_pairs={{0,2},{2,0},{1,3},{3,1},{4,6},{6,4},{5,7},{7,5},{8,10},{10,8},{9,1... | collective-permute-start | bytes 196616 | tf_op jit(solution)/shard_map/ppermute | solution.py:279
  1.2 0.1 collective-permute-start.1
  1.3 2.2 %fetch.1.weight_ref = bf16[2,1024,1024]{2,1,0:T(8,128)(2,1)S(1)} custom-call(bf16[1024,1024]{1,0:T(8,128)(2,1)} %sens_ref_hbm.1, bf16[1024,1024]{1,0:T(8,128)(2,1)} %sens_val_hbm.1, bf16[1024,1024]{1,0:T(8,128)(2,1)} %vid_ref_hbm.1, bf16[1024,1024]{1,0:T(8,128)(2,1)} %vid_val_hbm.1), custom_call_target="tpu_custom_call" | custom-call | flops 1073741824 | bytes 8388608 | tf_op jit(solution)/shard_map/fetch/pallas_call | solution.py:45
  3.5 0.0 collective-permute-done.other_sensor_ref
  3.5 0.0 collective-permute-done.1.other_video_ref
  3.6 0.0 copy-done.2
  3.6 0.0 copy-done.3
  3.6 0.9 %project.1 = bf16[16,1,2,32,128]{4,3,2,1,0:T(8,128)(2,1)S(1)} custom-call(bf16[32,1024]{1,0:T(8,128)(2,1)S(1)} %copy-done.2, bf16[32,1024]{1,0:T(8,128)(2,1)S(1)} %copy-done.3, bf16[32,1024]{1,0:T(8,128)(2,1)S(1)} %collective-permute-done.other_sensor_ref, bf16[32,1024]{1,0:T(8,128)(2,1)S(1)} %collective-permute-done.1.other_video_ref, ...), custom_call_target="tpu_custom_call" | custom-call | flops 268435456 | bytes 4194304 | tf_op jit(solution)/shard_map/project/pallas_call | solution.py:89
  4.5 17.6 %all_to_all.10 = bf16[32,32,128]{2,1,0:T(8,128)(2,1)S(1)} all-to-all(bf16[32,32,128]{2,1,0:T(8,128)(2,1)S(1)} %bitcast.6), channel_id=1, replica_groups=mesh['cell'=8,'core'=2,'quarter'=2] {'cell','quarter','core'}, dimensions={0} | all-to-all | bytes 524288 | tf_op jit(solution)/shard_map/all_to_all | solution.py:282
  22.1 0.0 collective-permute-start.2
  22.2 1.0 %attend_near.1 = (f32[2,512,128]{2,1,0:T(8,128)S(1)}, f32[2,512,128]{2,1,0:T(8,128)S(1)}) custom-call(bf16[16,2,32,128]{3,2,1,0:T(8,128)(2,1)S(1)} %bitcast.8, bf16[16,2,32,128]{3,2,1,0:T(8,128)(2,1)S(1)} %bitcast.9), custom_call_target="tpu_custom_call" | custom-call | flops 2147483648 | bytes 524288 | tf_op jit(solution)/shard_map/attend_near/pallas_call | solution.py:190
  23.2 0.5 %collective-permute-done.2 = bf16[32,32,128]{2,1,0:T(8,128)(2,1)S(1)} collective-permute-done((bf16[32,32,128]{2,1,0:T(8,128)(2,1)S(1)}, bf16[32,32,128]{2,1,0:T(8,128)(2,1)S(1)}, u32[]{:S(2)}, u32[]{:S(2)}) %collective-permute-start.2) | collective-permute-done | bytes 262176 | tf_op jit(solution)/shard_map/ppermute | solution.py:285
  23.7 0.0 copy-start
  23.7 0.0 copy-start.1
  23.7 0.0 copy-start.4
  23.7 0.0 copy-start.5
  23.7 1.6 %attend_far.1 = bf16[32,16,128]{2,1,0:T(8,128)(2,1)S(1)} custom-call(bf16[16,2,32,128]{3,2,1,0:T(8,128)(2,1)S(1)} %bitcast.10, bf16[16,2,32,128]{3,2,1,0:T(8,128)(2,1)S(1)} %bitcast.13, f32[2,512,128]{2,1,0:T(8,128)S(1)} %get-tuple-element.4.refs_2_, f32[2,512,128]{2,1,0:T(8,128)S(1)} %get-tuple-element.5.refs_3_), custom_call_target="tpu_custom_call" | custom-call | flops 2147483648 | bytes 524288 | tf_op jit(solution)/shard_map/attend_far/pallas_call | solution.py:204
  25.3 10.4 %all_to_all.11 = bf16[32,16,128]{2,1,0:T(8,128)(2,1)S(1)} all-to-all(bf16[32,16,128]{2,1,0:T(8,128)(2,1)S(1)} %attend_far.1), channel_id=1, replica_groups=mesh['cell'=8,'core'=2,'quarter'=2] {'cell','quarter','core'}, dimensions={0} | all-to-all | bytes 262144 | tf_op jit(solution)/shard_map/all_to_all | solution.py:296
  35.7 0.0 copy-done
  35.8 0.0 copy-done.1
  35.8 0.0 copy-done.4
  35.8 0.0 copy-done.5
  35.8 1.6 %finish.1 = (bf16[32,1024]{1,0:T(8,128)(2,1)}, bf16[32,1024]{1,0:T(8,128)(2,1)}) custom-call(bf16[16,2,16,128]{3,2,1,0:T(8,128)(2,1)S(1)} %bitcast.7, bf16[32,1024]{1,0:T(8,128)(2,1)S(1)} %copy-done.2, bf16[32,1024]{1,0:T(8,128)(2,1)S(1)} %copy-done.3, f32[1,1024]{1,0:T(1,128)S(1)} %bitcast.11, f32[1,1024]{1,0:T(1,128)S(1)} %bitcast.12, ...), custom_call_target="tpu_custom_call" | custom-call | flops 134217728 | bytes 4194304 | tf_op jit(solution)/shard_map/finish/pallas_call | solution.py:251
Async XLA Ops:
  0.6 2.9 %copy-start.2 = (bf16[32,1024]{1,0:T(8,128)(2,1)S(1)}, bf16[32,1024]{1,0:T(8,128)(2,1)}, u32[]{:S(2)}) copy-start(bf16[32,1024]{1,0:T(8,128)(2,1)} %sensor_ref.3) | copy-start | bytes 196612
  0.6 2.9 %copy-start.3 = (bf16[32,1024]{1,0:T(8,128)(2,1)S(1)}, bf16[32,1024]{1,0:T(8,128)(2,1)}, u32[]{:S(2)}) copy-start(bf16[32,1024]{1,0:T(8,128)(2,1)} %video_ref.3) | copy-start | bytes 196612
  0.7 2.9 %collective-permute-start = (bf16[32,1024]{1,0:T(8,128)(2,1)}, bf16[32,1024]{1,0:T(8,128)(2,1)S(1)}, u32[]{:S(2)}, u32[]{:S(2)}) collective-permute-start(bf16[32,1024]{1,0:T(8,128)(2,1)} %sensor_ref.3), channel_id=1, source_target_pairs={{0,2},{2,0},{1,3},{3,1},{4,6},{6,4},{5,7},{7,5},{8,10},{10,8},{9,1... | collective-permute-start | bytes 196616 | tf_op jit(solution)/shard_map/ppermute | solution.py:279
  1.2 2.3 %collective-permute-start.1 = (bf16[32,1024]{1,0:T(8,128)(2,1)}, bf16[32,1024]{1,0:T(8,128)(2,1)S(1)}, u32[]{:S(2)}, u32[]{:S(2)}) collective-permute-start(bf16[32,1024]{1,0:T(8,128)(2,1)} %video_ref.3), channel_id=1, source_target_pairs={{0,2},{2,0},{1,3},{3,1},{4,6},{6,4},{5,7},{7,5},{8,10},{10,8},{9,1... | collective-permute-start | bytes 196616 | tf_op jit(solution)/shard_map/ppermute | solution.py:279
  22.1 1.5 %collective-permute-start.2 = (bf16[32,32,128]{2,1,0:T(8,128)(2,1)S(1)}, bf16[32,32,128]{2,1,0:T(8,128)(2,1)S(1)}, u32[]{:S(2)}, u32[]{:S(2)}) collective-permute-start(bf16[32,32,128]{2,1,0:T(8,128)(2,1)S(1)} %all_to_all.10), channel_id=1, source_target_pairs={{0,2},{2,0},{1,3},{3,1},{4,6},{6,4},{5,7},{7,5},{8,10},{10,8},{9,1... | collective-permute-start | bytes 786440 | tf_op jit(solution)/shard_map/ppermute | solution.py:285
  23.7 12.1 %copy-start = (bf16[1024,1024]{1,0:T(8,128)(2,1)S(1)}, bf16[1024,1024]{1,0:T(8,128)(2,1)}, u32[]{:S(2)}) copy-start(bf16[1024,1024]{1,0:T(8,128)(2,1)} %sens_out_ref.1) | copy-start | bytes 6291460
  23.7 12.1 %copy-start.1 = (bf16[1024,1024]{1,0:T(8,128)(2,1)S(1)}, bf16[1024,1024]{1,0:T(8,128)(2,1)}, u32[]{:S(2)}) copy-start(bf16[1024,1024]{1,0:T(8,128)(2,1)} %vid_out_ref.1) | copy-start | bytes 6291460
  23.7 12.1 %copy-start.4 = (f32[1024]{0:T(1024)S(1)}, f32[1024]{0:T(1024)}, u32[]{:S(2)}) copy-start(f32[1024]{0:T(1024)} %param.18) | copy-start | bytes 12292
  23.7 12.1 %copy-start.5 = (f32[1024]{0:T(1024)S(1)}, f32[1024]{0:T(1024)}, u32[]{:S(2)}) copy-start(f32[1024]{0:T(1024)} %param.19) | copy-start | bytes 12292

commit v5 on v4

--- a/solution.py
+++ b/solution.py
@@ -156,21 +156,20 @@
         chips = slice(start // rows, (start + block) // rows)
         part = slice(start, start + block)
         ends = []
-        for stream in range(STREAMS):
-            query = query_ref[chips, stream, :, :].reshape(block, pair)
-            scores = scored(query, boths[stream])
+        queries = [query_ref[chips, s, :, :].reshape(block, pair) for s in range(STREAMS)]
+        found = [scored(query, both) for query, both in zip(queries, boths)]
+        for stream, scores in enumerate(found):
             near_top = top_ref[stream, part, :]
-            top = jnp.maximum(near_top[:, :1], jnp.max(scores, axis=1, keepdims=True))
-            weights = jnp.exp2((scores - top) * factor).astype(out_ref.dtype)
+            top = jnp.maximum(near_top, jnp.max(scores, axis=1, keepdims=True))
+            wide = jnp.concatenate([top] * (scores.shape[1] // pair), axis=1)
+            weights = jnp.exp2((scores - wide) * factor).astype(out_ref.dtype)
             mixed = mixed_ref[stream, part, :] * jnp.exp2((near_top - top) * factor)
-            mixed = mixed + jnp.dot(
-                weights, values[stream], preferred_element_type=jnp.float32
+            ends.append(
+                mixed + jnp.dot(weights, values[stream], preferred_element_type=jnp.float32)
             )
-            if stream == 0:
-                ends.append(half_turn(mixed) / mixed)
-            else:
-                ends.append(mixed / half_turn(mixed))
-        both = jnp.where(low, ends[0], ends[1]).astype(out_ref.dtype)
+        turned = [half_turn(end) for end in ends]
+        total = jnp.where(low, ends[0], turned[1])
+        both = (jnp.where(low, turned[0], ends[1]) / total).astype(out_ref.dtype)
         devices = slice(start // half, (start + block) // half)
         out_ref[devices, :, :] = both.reshape(block // half, half, pair)
 

time: 37.6 us -> 36.9 us (0.981)
  Pallas kernels: 7.44 us -> 6.81 us
    pallas_call x1, Pallas kernels: 1.63 us -> 1 us  [attend_far(): pl.pallas_call(lambda *refs: attend_far_kernel(factor, *refs), name='atte...]
where the time goes in v5:
time: 36.9 us; the launch traced here: 36.7 us
  blocking collectives  28.1 us (76%)
  Pallas kernels  6.81 us (18%)
  between operations  0.73 us (2%)
  starting transfers between devices  0.64 us (2%)
  waiting for transfers between devices  0.49 us (1%)
    all_to_all x1, blocking collectives, local(): lax.all_to_all(sent.reshape(devices, rows, pair), ORDER, split_axis=0, co...  17.6 us
    all_to_all x1, blocking collectives, local(): lax.all_to_all(mixed, ORDER, split_axis=0, concat_axis=0, tiled=True)  10.4 us
    pallas_call x1, Pallas kernels, fetch(): pl.pallas_call(fetch_kernel, name='fetch', out_shape=jax.ShapeDtypeStruct...  2.24 us
    pallas_call x1, Pallas kernels, finish(): pl.pallas_call(finish_kernel, name='finish', out_shape=(shape, shape), in...  1.61 us
    pallas_call x1, Pallas kernels, attend_near(): pl.pallas_call(lambda *refs: attend_near_kernel(factor, *refs), name='att...  1.04 us
    pallas_call x1, Pallas kernels, attend_far(): pl.pallas_call(lambda *refs: attend_far_kernel(factor, *refs), name='atte...  1 us
    pallas_call x1, Pallas kernels, project(): pl.pallas_call(project_kernel, name='project', out_shape=jax.ShapeDtypeSt...  0.92 us
  transfers between devices with their start and end apart: 3, of which 1 were waited for; matrix products, arithmetic and copies ran while one was open for 0% of the time, Pallas kernels for 9%

profile of v5, /device:TPU:0, one launch (start us, length us, event | category | flops | bytes accessed | tf_op | source)
XLA Modules:
  0.0 36.7 jit_solution(3590625528534802866)
XLA Ops:
  0.6 0.0 copy-start.2
  0.6 0.0 copy-start.3
  0.7 0.6 %collective-permute-start = (bf16[32,1024]{1,0:T(8,128)(2,1)}, bf16[32,1024]{1,0:T(8,128)(2,1)S(1)}, u32[]{:S(2)}, u32[]{:S(2)}) collective-permute-start(bf16[32,1024]{1,0:T(8,128)(2,1)} %sensor_ref.3), channel_id=1, source_target_pairs={{0,2},{2,0},{1,3},{3,1},{4,6},{6,4},{5,7},{7,5},{8,10},{10,8},{9,1... | collective-permute-start | bytes 196616 | tf_op jit(solution)/shard_map/ppermute | solution.py:278
  1.2 0.1 collective-permute-start.1
  1.3 2.2 %fetch.1.weight_ref = bf16[2,1024,1024]{2,1,0:T(8,128)(2,1)S(1)} custom-call(bf16[1024,1024]{1,0:T(8,128)(2,1)} %sens_ref_hbm.1, bf16[1024,1024]{1,0:T(8,128)(2,1)} %sens_val_hbm.1, bf16[1024,1024]{1,0:T(8,128)(2,1)} %vid_ref_hbm.1, bf16[1024,1024]{1,0:T(8,128)(2,1)} %vid_val_hbm.1), custom_call_target="tpu_custom_call" | custom-call | flops 1073741824 | bytes 8388608 | tf_op jit(solution)/shard_map/fetch/pallas_call | solution.py:45
  3.5 0.0 collective-permute-done.other_sensor_ref
  3.5 0.0 collective-permute-done.1.other_video_ref
  3.6 0.0 copy-done.2
  3.6 0.0 copy-done.3
  3.6 0.9 %project.1 = bf16[16,1,2,32,128]{4,3,2,1,0:T(8,128)(2,1)S(1)} custom-call(bf16[32,1024]{1,0:T(8,128)(2,1)S(1)} %copy-done.2, bf16[32,1024]{1,0:T(8,128)(2,1)S(1)} %copy-done.3, bf16[32,1024]{1,0:T(8,128)(2,1)S(1)} %collective-permute-done.other_sensor_ref, bf16[32,1024]{1,0:T(8,128)(2,1)S(1)} %collective-permute-done.1.other_video_ref, ...), custom_call_target="tpu_custom_call" | custom-call | flops 268435456 | bytes 4194304 | tf_op jit(solution)/shard_map/project/pallas_call | solution.py:89
  4.5 17.6 %all_to_all.10 = bf16[32,32,128]{2,1,0:T(8,128)(2,1)S(1)} all-to-all(bf16[32,32,128]{2,1,0:T(8,128)(2,1)S(1)} %bitcast.6), channel_id=1, replica_groups=mesh['cell'=8,'core'=2,'quarter'=2] {'cell','quarter','core'}, dimensions={0} | all-to-all | bytes 524288 | tf_op jit(solution)/shard_map/all_to_all | solution.py:281
  22.1 0.0 collective-permute-start.2
  22.2 1.0 %attend_near.1 = (f32[2,512,128]{2,1,0:T(8,128)S(1)}, f32[2,512,128]{2,1,0:T(8,128)S(1)}) custom-call(bf16[16,2,32,128]{3,2,1,0:T(8,128)(2,1)S(1)} %bitcast.8, bf16[16,2,32,128]{3,2,1,0:T(8,128)(2,1)S(1)} %bitcast.9), custom_call_target="tpu_custom_call" | custom-call | flops 2147483648 | bytes 524288 | tf_op jit(solution)/shard_map/attend_near/pallas_call | solution.py:189
  23.2 0.5 %collective-permute-done.2 = bf16[32,32,128]{2,1,0:T(8,128)(2,1)S(1)} collective-permute-done((bf16[32,32,128]{2,1,0:T(8,128)(2,1)S(1)}, bf16[32,32,128]{2,1,0:T(8,128)(2,1)S(1)}, u32[]{:S(2)}, u32[]{:S(2)}) %collective-permute-start.2) | collective-permute-done | bytes 262176 | tf_op jit(solution)/shard_map/ppermute | solution.py:284
  23.7 0.0 copy-start
  23.7 0.0 copy-start.1
  23.7 0.0 copy-start.4
  23.7 0.0 copy-start.5
  23.7 1.0 %attend_far.1 = bf16[32,16,128]{2,1,0:T(8,128)(2,1)S(1)} custom-call(bf16[16,2,32,128]{3,2,1,0:T(8,128)(2,1)S(1)} %bitcast.10, bf16[16,2,32,128]{3,2,1,0:T(8,128)(2,1)S(1)} %bitcast.13, f32[2,512,128]{2,1,0:T(8,128)S(1)} %get-tuple-element.4.refs_2_, f32[2,512,128]{2,1,0:T(8,128)S(1)} %get-tuple-element.5.refs_3_), custom_call_target="tpu_custom_call" | custom-call | flops 2147483648 | bytes 524288 | tf_op jit(solution)/shard_map/attend_far/pallas_call | solution.py:203
  24.7 10.4 %all_to_all.11 = bf16[32,16,128]{2,1,0:T(8,128)(2,1)S(1)} all-to-all(bf16[32,16,128]{2,1,0:T(8,128)(2,1)S(1)} %attend_far.1), channel_id=1, replica_groups=mesh['cell'=8,'core'=2,'quarter'=2] {'cell','quarter','core'}, dimensions={0} | all-to-all | bytes 262144 | tf_op jit(solution)/shard_map/all_to_all | solution.py:295
  35.1 0.0 copy-done
  35.1 0.0 copy-done.1
  35.1 0.0 copy-done.4
  35.1 0.0 copy-done.5
  35.1 1.6 %finish.1 = (bf16[32,1024]{1,0:T(8,128)(2,1)}, bf16[32,1024]{1,0:T(8,128)(2,1)}) custom-call(bf16[16,2,16,128]{3,2,1,0:T(8,128)(2,1)S(1)} %bitcast.7, bf16[32,1024]{1,0:T(8,128)(2,1)S(1)} %copy-done.2, bf16[32,1024]{1,0:T(8,128)(2,1)S(1)} %copy-done.3, f32[1,1024]{1,0:T(1,128)S(1)} %bitcast.11, f32[1,1024]{1,0:T(1,128)S(1)} %bitcast.12, ...), custom_call_target="tpu_custom_call" | custom-call | flops 134217728 | bytes 4194304 | tf_op jit(solution)/shard_map/finish/pallas_call | solution.py:250
Async XLA Ops:
  0.6 2.9 %copy-start.2 = (bf16[32,1024]{1,0:T(8,128)(2,1)S(1)}, bf16[32,1024]{1,0:T(8,128)(2,1)}, u32[]{:S(2)}) copy-start(bf16[32,1024]{1,0:T(8,128)(2,1)} %sensor_ref.3) | copy-start | bytes 196612
  0.6 2.9 %copy-start.3 = (bf16[32,1024]{1,0:T(8,128)(2,1)S(1)}, bf16[32,1024]{1,0:T(8,128)(2,1)}, u32[]{:S(2)}) copy-start(bf16[32,1024]{1,0:T(8,128)(2,1)} %video_ref.3) | copy-start | bytes 196612
  0.7 2.9 %collective-permute-start = (bf16[32,1024]{1,0:T(8,128)(2,1)}, bf16[32,1024]{1,0:T(8,128)(2,1)S(1)}, u32[]{:S(2)}, u32[]{:S(2)}) collective-permute-start(bf16[32,1024]{1,0:T(8,128)(2,1)} %sensor_ref.3), channel_id=1, source_target_pairs={{0,2},{2,0},{1,3},{3,1},{4,6},{6,4},{5,7},{7,5},{8,10},{10,8},{9,1... | collective-permute-start | bytes 196616 | tf_op jit(solution)/shard_map/ppermute | solution.py:278
  1.2 2.3 %collective-permute-start.1 = (bf16[32,1024]{1,0:T(8,128)(2,1)}, bf16[32,1024]{1,0:T(8,128)(2,1)S(1)}, u32[]{:S(2)}, u32[]{:S(2)}) collective-permute-start(bf16[32,1024]{1,0:T(8,128)(2,1)} %video_ref.3), channel_id=1, source_target_pairs={{0,2},{2,0},{1,3},{3,1},{4,6},{6,4},{5,7},{7,5},{8,10},{10,8},{9,1... | collective-permute-start | bytes 196616 | tf_op jit(solution)/shard_map/ppermute | solution.py:278
  22.1 1.5 %collective-permute-start.2 = (bf16[32,32,128]{2,1,0:T(8,128)(2,1)S(1)}, bf16[32,32,128]{2,1,0:T(8,128)(2,1)S(1)}, u32[]{:S(2)}, u32[]{:S(2)}) collective-permute-start(bf16[32,32,128]{2,1,0:T(8,128)(2,1)S(1)} %all_to_all.10), channel_id=1, source_target_pairs={{0,2},{2,0},{1,3},{3,1},{4,6},{6,4},{5,7},{7,5},{8,10},{10,8},{9,1... | collective-permute-start | bytes 786440 | tf_op jit(solution)/shard_map/ppermute | solution.py:284
  23.7 11.4 %copy-start = (bf16[1024,1024]{1,0:T(8,128)(2,1)S(1)}, bf16[1024,1024]{1,0:T(8,128)(2,1)}, u32[]{:S(2)}) copy-start(bf16[1024,1024]{1,0:T(8,128)(2,1)} %sens_out_ref.1) | copy-start | bytes 6291460
  23.7 11.4 %copy-start.1 = (bf16[1024,1024]{1,0:T(8,128)(2,1)S(1)}, bf16[1024,1024]{1,0:T(8,128)(2,1)}, u32[]{:S(2)}) copy-start(bf16[1024,1024]{1,0:T(8,128)(2,1)} %vid_out_ref.1) | copy-start | bytes 6291460
  23.7 11.4 %copy-start.4 = (f32[1024]{0:T(1024)S(1)}, f32[1024]{0:T(1024)}, u32[]{:S(2)}) copy-start(f32[1024]{0:T(1024)} %param.18) | copy-start | bytes 12292
  23.7 11.4 %copy-start.5 = (f32[1024]{0:T(1024)S(1)}, f32[1024]{0:T(1024)}, u32[]{:S(2)}) copy-start(f32[1024]{0:T(1024)} %param.19) | copy-start | bytes 12292
